TPU v7x, 8 devices: a whole 2x2x1 slice. The times are simulated.
8 devices in a mesh: dp: 2 (over z, y), ep: 4 (over x, core).
Axes of the slice: x: 2, y: 2, z: 1, core: 2. Of those that a mesh axis runs over, the one named last changes fastest.
Arguments:
- h0: bfloat16 [8, 256, 2048], P(('dp', 'ep')), parts along dimension 0
- idx: int32 [8, 256, 6], P(('dp', 'ep')), parts along dimension 0
- slot: int32 [8, 256, 6], P(('dp', 'ep')), parts along dimension 0
- ln_attn: bfloat16 [2048], replicated
- wq: bfloat16 [2048, 2048], replicated
- wk: bfloat16 [2048, 2048], replicated
- wv: bfloat16 [2048, 2048], replicated
- wo: bfloat16 [2048, 2048], replicated
- ln_ffn: bfloat16 [2048], replicated
- ws1: bfloat16 [2048, 2816], replicated
- ws3: bfloat16 [2048, 2816], replicated
- ws2: bfloat16 [2816, 2048], replicated
- ln_moe: bfloat16 [2048], replicated
- wr: bfloat16 [2048, 64], replicated
- ue1: bfloat16 [64, 2048, 1408], P('ep')
- ue3: bfloat16 [64, 2048, 1408], P('ep')
- ue2: bfloat16 [64, 1408, 2048], P('ep')
Outputs:
- output: bfloat16 [8, 256, 2048], P(('dp', 'ep')), parts along dimension 0
There are 2 independent parts. A program takes and returns all parts, laid end to end along the dimension named above; an argument that names none is the same for every part.
All inputs are finite; a program needn't handle non-finite values.
Results may differ from a plain program's by a relative error of at most 0.00930081.
Values are sent between devices in bfloat16 or wider.
A program may use at most 1.5 GiB of HBM per device.

v0:
```python
import jax
import jax.numpy as jnp
from jax import lax
from jax.sharding import PartitionSpec as P

HEAD = 128
EPS = 1e-6
CAP_FACTOR = 2


def _mm(form, a, b):
    return jnp.einsum(form, a, b, preferred_element_type=jnp.float32)


def _rms(x, w):
    xf = x.astype(jnp.float32)
    r = lax.rsqrt(jnp.mean(xf * xf, axis=-1, keepdims=True) + EPS)
    return (xf * r * w.astype(jnp.float32)).astype(jnp.bfloat16)


def _rope(x):
    s, half = x.shape[1], x.shape[-1] // 2
    freq = 10000.0 ** (-jnp.arange(half, dtype=jnp.float32) / half)
    ang = jnp.arange(s, dtype=jnp.float32)[:, None] * freq[None, :]
    c = jnp.cos(ang)[None, :, None, :]
    sn = jnp.sin(ang)[None, :, None, :]
    x1, x2 = x[..., :half], x[..., half:]
    return jnp.concatenate([x1 * c - x2 * sn, x2 * c + x1 * sn], axis=-1)


def _dense(h0, ln_attn, wq, wk, wv, wo, ln_ffn, ws1, ws3, ws2):
    b, s, _ = h0.shape
    nh = wq.shape[1] // HEAD
    x1 = _rms(h0, ln_attn)
    q = _rope(_mm('bsd,de->bse', x1, wq).reshape(b, s, nh, HEAD)).astype(jnp.bfloat16)
    k = _rope(_mm('bsd,de->bse', x1, wk).reshape(b, s, nh, HEAD)).astype(jnp.bfloat16)
    v = _mm('bsd,de->bse', x1, wv).astype(jnp.bfloat16).reshape(b, s, nh, HEAD)
    sc = _mm('bqhe,bkhe->bhqk', q, k) * HEAD ** -0.5
    causal = jnp.arange(s)[:, None] >= jnp.arange(s)[None, :]
    p = jax.nn.softmax(jnp.where(causal, sc, -1e30), axis=-1).astype(jnp.bfloat16)
    o = _mm('bhqk,bkhe->bqhe', p, v).astype(jnp.bfloat16).reshape(b, s, nh * HEAD)
    a = (h0.astype(jnp.float32) + _mm('bse,ed->bsd', o, wo)).astype(jnp.bfloat16)
    x2 = _rms(a, ln_ffn)
    hs = (jax.nn.silu(_mm('bsd,df->bsf', x2, ws1)) * _mm('bsd,df->bsf', x2, ws3)).astype(jnp.bfloat16)
    return a, _mm('bsf,fd->bsd', hs, ws2)


def _experts(x, ue1, ue3, ue2):
    he = (jax.nn.silu(_mm('gecd,edf->egcf', x, ue1)) * _mm('gecd,edf->egcf', x, ue3)).astype(jnp.bfloat16)
    return _mm('egcf,efd->gecd', he, ue2).astype(jnp.bfloat16)


def _gate(u, wr, gi):
    lg = _mm('td,de->te', u, wr)
    hit = gi[..., None] == jnp.arange(wr.shape[1], dtype=gi.dtype)
    return jax.nn.softmax(jnp.sum(jnp.where(hit, lg[:, None, :], 0.0), axis=-1), axis=-1)


def _route(q, gate, n):
    hit = q[..., None] == jnp.arange(n, dtype=q.dtype)
    disp = jnp.any(hit, axis=-2).astype(jnp.bfloat16)
    comb = jnp.sum(jnp.where(hit, gate[..., None], 0.0), axis=-2)
    return disp, comb


def _parts(c):
    hi = c.astype(jnp.bfloat16)
    r = c - hi.astype(jnp.float32)
    mid = r.astype(jnp.bfloat16)
    lo = (r - mid.astype(jnp.float32)).astype(jnp.bfloat16)
    return hi, mid, lo


def solution(mesh):
    g_ = mesh.shape['ep']
    rows = P(('dp', 'ep'))
    rep = P()

    def local(h0, idx, slot, ln_attn, wq, wk, wv, wo, ln_ffn, ws1, ws3, ws2, ln_moe, wr, ue1, ue3, ue2):
        b, s, d = h0.shape
        top = idx.shape[-1]
        el = ue1.shape[0]
        ne = el * g_
        t = b * s
        cap = CAP_FACTOR * t * top // ne
        a, fo = _dense(h0, ln_attn, wq, wk, wv, wo, ln_ffn, ws1, ws3, ws2)
        u = _rms(h0, ln_moe).reshape(t, d)
        gi = idx.reshape(t, top)
        sl = slot.reshape(t, top)
        gate = _gate(u, wr, gi)
        disp, comb = _route(gi * cap + sl, gate, ne * cap)
        send = _mm('tr,td->rd', disp, u).astype(jnp.bfloat16).reshape(g_, el, cap, d)
        recv = lax.all_to_all(send, 'ep', 0, 0, tiled=True)
        y = _experts(recv, ue1, ue3, ue2)
        back = lax.all_to_all(y, 'ep', 0, 0, tiled=True).reshape(ne * cap, d)
        m = sum(_mm('tr,rd->td', p, back) for p in _parts(comb))
        out = a.astype(jnp.float32) + fo + m.reshape(b, s, d)
        return out.astype(jnp.bfloat16)

    specs = (rows, rows, rows) + (rep,) * 11 + (P('ep'), P('ep'), P('ep'))
    return jax.shard_map(local, mesh=mesh, in_specs=specs, out_specs=rows, check_vma=False)
```

profile of v0, /device:TPU:0, one launch (start us, length us, event | category | flops | bytes accessed | tf_op | source)
XLA Modules:
  0.0 464.3 jit_solution(8968080525519437311)
XLA Ops:
  0.0 1.6 fusion.28
  1.6 0.7 bitcast_add_fusion
  2.3 0.6 copy-done.3
  2.9 4.2 fusion.7
  7.1 0.7 convert_element_type.103
  7.8 7.8 %convolution_convert_fusion = bf16[3072,2048]{1,0:T(8,128)(2,1)} fusion(pred[256,3072]{1,0:T(8,128)(4,1)S(1)} %fusion.7, bf16[1,256,2048]{2,1,0:T(8,128)(2,1)} %param.17, f32[2048]{0:T(1024)S(1)} %convert_element_type.103, f32[256]{0:T(256)S(1)} %add_rsqrt_fusion.1), kind=kOutput, calls=%fused_computation.12 | convolution fusion | flops 3229614080 | bytes 14427136 | tf_op jit(solution)/shard_map/tr,td->rd/dot_general | solution.py:12
  15.6 6.6 %all-to-all-start = ((bf16[4,16,48,2048]{3,2,1,0:T(8,128)(2,1)}), bf16[4,16,48,2048]{3,2,1,0:T(8,128)(2,1)}, u32[]{:S(2)}, u32[]{:S(2)}) async-start(bf16[4,16,48,2048]{3,2,1,0:T(8,128)(2,1)} %bitcast.100), calls=%async_computation | async-start | bytes 25165824 | tf_op jit(solution)/shard_map/all_to_all | solution.py:93
  22.2 0.6 copy.79
  22.8 138.2 %all-to-all-done = bf16[4,16,48,2048]{3,2,1,0:T(8,128)(2,1)} async-done(((bf16[4,16,48,2048]{3,2,1,0:T(8,128)(2,1)}), bf16[4,16,48,2048]{3,2,1,0:T(8,128)(2,1)}, u32[]{:S(2)}, u32[]{:S(2)}) %all-to-all-start) | async-done | bytes 12582944 | tf_op jit(solution)/shard_map/all_to_all | solution.py:93
  161.1 40.9 %fusion.3 = f32[16,4,48,1408]{3,2,1,0:T(8,128)} fusion(bf16[16,2048,1408]{2,1,0:T(8,128)(2,1)} %param.32, bf16[4,16,48,2048]{3,2,1,0:T(8,128)(2,1)} %all-to-all-done), kind=kOutput, calls=%fused_computation.3 | convolution fusion | flops 17716740096 | bytes 122159104 | tf_op jit(solution)/shard_map/gecd,edf->egcf/dot_general | solution.py:12
  201.9 46.3 %multiply_convert_fusion = bf16[16,4,48,1408]{3,2,1,0:T(8,128)(2,1)} fusion(f32[16,4,48,1408]{3,2,1,0:T(8,128)} %fusion.3, bf16[16,2048,1408]{2,1,0:T(8,128)(2,1)} %param.31, bf16[4,16,48,2048]{3,2,1,0:T(8,128)(2,1)} %all-to-all-done), kind=kOutput, calls=%fused_computation.10 | convolution fusion | flops 17742692352 | bytes 130809856 | tf_op jit(solution)/shard_map/gecd,edf->egcf/dot_general | solution.py:12
  248.2 38.6 %convert_bitcast_fusion = bf16[4,16,48,2048]{3,2,0,1:T(8,128)(2,1)} fusion(bf16[16,4,48,1408]{3,2,1,0:T(8,128)(2,1)} %multiply_convert_fusion, bf16[16,1408,2048]{2,1,0:T(8,128)(2,1)} %param.33), kind=kOutput, calls=%fused_computation.11 | convolution fusion | flops 17723031552 | bytes 113508352 | tf_op jit(solution)/shard_map/egcf,efd->gecd/dot_general | solution.py:12
  286.8 10.7 %copy.59 = bf16[4,16,48,2048]{3,2,1,0:T(8,128)(2,1)} copy(bf16[4,16,48,2048]{3,2,0,1:T(8,128)(2,1)} %convert_bitcast_fusion) | data formatting | bytes 25165824 | tf_op jit(solution)/shard_map/convert_element_type | solution.py:50
  297.6 6.7 %all-to-all-start.1 = ((bf16[4,16,48,2048]{3,2,1,0:T(8,128)(2,1)}), bf16[4,16,48,2048]{3,2,1,0:T(8,128)(2,1)}, u32[]{:S(2)}, u32[]{:S(2)}) async-start(bf16[4,16,48,2048]{3,2,1,0:T(8,128)(2,1)} %copy.59), calls=%async_computation.1 | async-start | bytes 25165824 | tf_op jit(solution)/shard_map/all_to_all | solution.py:95
  304.2 5.8 %convolution_convert_fusion.1 = bf16[256,2048]{1,0:T(8,128)(2,1)S(1)} fusion(bf16[2048,2048]{1,0:T(8,128)(2,1)} %param.23, bf16[1,256,2048]{2,1,0:T(8,128)(2,1)S(1)} %copy-done.1, f32[2048]{0:T(1024)S(1)} %convert_element_type.91, f32[256]{0:T(256)S(1)} %add_rsqrt_fusion.1), kind=kOutput, calls=%fused_computation.37 | convolution fusion | flops 2150105088 | bytes 10494976 | tf_op jit(solution)/shard_map/bsd,de->bse/dot_general | solution.py:12
  310.5 12.4 %copy.68 = bf16[2048,2048]{1,0:T(8,128)(2,1)} copy(bf16[2048,2048]{0,1:T(8,128)(2,1)} %bitcast.103) | data formatting | bytes 16777216 | tf_op jit(solution)/shard_map/bsd,de->bse/dot_general | solution.py:12
  322.9 12.3 %copy.67 = bf16[2048,2048]{1,0:T(8,128)(2,1)} copy(bf16[2048,2048]{0,1:T(8,128)(2,1)} %bitcast.104) | data formatting | bytes 16777216 | tf_op jit(solution)/shard_map/bsd,de->bse/dot_general | solution.py:12
  336.2 5.8 %convolution_bitcast_fusion.2 = f32[1,256,16,128]{1,3,2,0:T(8,128)S(1)} fusion(bf16[16,128,2048]{2,1,0:T(8,128)(2,1)} %bitcast.106, bf16[1,256,2048]{2,1,0:T(8,128)(2,1)S(1)} %copy-done.1, f32[2048]{0:T(1024)S(1)} %convert_element_type.91, f32[256]{0:T(256)S(1)} %add_rsqrt_fusion.1), kind=kOutput, calls=%fused_computation.53 | convolution fusion | flops 2149580800 | bytes 11543552 | tf_op jit(solution)/shard_map/bsd,de->bse/dot_general | solution.py:12
  342.1 5.8 %convolution_bitcast_fusion.3 = f32[1,256,16,128]{1,3,2,0:T(8,128)S(1)} fusion(bf16[16,128,2048]{2,1,0:T(8,128)(2,1)} %bitcast.105, bf16[1,256,2048]{2,1,0:T(8,128)(2,1)S(1)} %copy-done.1, f32[2048]{0:T(1024)S(1)} %convert_element_type.91, f32[256]{0:T(256)S(1)} %add_rsqrt_fusion.1), kind=kOutput, calls=%fused_computation.54 | convolution fusion | flops 2149580800 | bytes 11543552 | tf_op jit(solution)/shard_map/bsd,de->bse/dot_general | solution.py:12
  347.9 0.7 fusion.51
  348.6 0.8 fusion.39
  349.4 1.7 fusion.71
  351.1 0.5 fusion.36
  351.7 1.7 slice-done.1
  353.4 2.5 fusion.29
  355.9 4.2 select_reduce_fusion
  360.1 4.9 %fusion.55 = f32[256,2816]{1,0:T(8,128)} fusion(bf16[2048,2816]{1,0:T(8,128)(2,1)S(1)} %bitcast.111, bf16[1,256,2048]{2,1,0:T(8,128)(2,1)S(1)} %get-tuple-element.16, f32[2048]{0:T(1024)S(1)} %convert_element_type.100, f32[256]{0:T(256)S(1)} %add_rsqrt_fusion), kind=kOutput, calls=%fused_computation.78 | convolution fusion | flops 2954887168 | bytes 15475712 | tf_op jit(solution)/shard_map/bsd,df->bsf/dot_general | solution.py:12
  365.0 16.8 %convert_add_fusion = f32[1,256,2048]{2,1,0:T(8,128)} fusion(bf16[1,256,2048]{2,1,0:T(8,128)(2,1)} %copy-done.2, bf16[2816,2048]{1,0:T(8,128)(2,1)} %param.28, bf16[2048,2816]{1,0:T(8,128)(2,1)} %param.27, f32[256,2816]{1,0:T(8,128)} %fusion.55, f32[2048]{0:T(1024)S(1)} %convert_element_type.100, f32[256]{0:T(256)S(1)} %add_rsqrt_fusion), kind=kOutput, calls=%fused_computation.23 | convolution fusion | flops 5913051136 | bytes 29107200 | tf_op jit(solution)/shard_map/bsf,fd->bsd/dot_general | solution.py:12
  381.9 60.1 %all-to-all-done.1 = bf16[4,16,48,2048]{3,2,1,0:T(8,128)(2,1)} async-done(((bf16[4,16,48,2048]{3,2,1,0:T(8,128)(2,1)}), bf16[4,16,48,2048]{3,2,1,0:T(8,128)(2,1)}, u32[]{:S(2)}, u32[]{:S(2)}) %all-to-all-start.1) | async-done | bytes 12582944 | tf_op jit(solution)/shard_map/all_to_all | solution.py:95
  442.0 6.4 %fusion.23 = f32[256,2048]{1,0:T(8,128)S(1)} fusion(bf16[3072,2048]{1,0:T(8,128)(2,1)} %bitcast.28, f32[256,3072]{1,0:T(8,128)S(1)} %select_reduce_fusion), kind=kOutput, calls=%fused_computation.41 | convolution fusion | flops 3222011904 | bytes 17825792 | tf_op jit(solution)/shard_map/tr,rd->td/dot_general | solution.py:12
  448.4 6.6 %convolution_add_fusion.1 = f32[256,2048]{1,0:T(8,128)S(1)} fusion(f32[256,2048]{1,0:T(8,128)S(1)} %fusion.23, bf16[3072,2048]{1,0:T(8,128)(2,1)} %bitcast.28, f32[256,3072]{1,0:T(8,128)S(1)} %select_reduce_fusion), kind=kOutput, calls=%fused_computation.34 | convolution fusion | flops 3224895488 | bytes 19922944 | tf_op jit(solution)/shard_map/tr,rd->td/dot_general | solution.py:12
  455.0 9.1 %fusion.18 = bf16[1,256,2048]{2,1,0:T(8,128)(2,1)} fusion(f32[1,256,2048]{2,1,0:T(8,128)S(1)} %copy-done.11, f32[256,2048]{1,0:T(8,128)S(1)} %convolution_add_fusion.1, bf16[3072,2048]{1,0:T(8,128)(2,1)} %bitcast.28, f32[256,3072]{1,0:T(8,128)S(1)} %select_reduce_fusion), kind=kOutput, calls=%fused_computation.35 | convolution fusion | flops 3228303360 | bytes 20971520 | tf_op jit(solution)/shard_map/tr,rd->td/dot_general | solution.py:12
  (47 shorter events, 1.6 us)
Async XLA Ops:
  0.0 335.2 %copy-start = (bf16[2048,64]{0,1:T(8,128)(2,1)S(1)}, bf16[2048,64]{0,1:T(8,128)(2,1)}, u32[]{:S(2)}) copy-start(bf16[2048,64]{0,1:T(8,128)(2,1)} %param.30) | copy-start | bytes 786436
  2.3 0.6 copy-start.3
  7.8 7.8 %copy-start.5 = (f32[2048]{0:T(1024)}, f32[2048]{0:T(1024)S(1)}, u32[]{:S(2)}) copy-start(f32[2048]{0:T(1024)S(1)} %convert_element_type.103) | copy-start | bytes 24580
  15.6 6.6 %copy-start.8 = (s32[1,256,6]{1,0,2:T(1,128)S(1)}, s32[1,256,6]{1,0,2:T(1,128)}, u32[]{:S(2)}) copy-start(s32[1,256,6]{1,0,2:T(1,128)} %param.18) | copy-start | bytes 18436
  15.6 7.2 %copy-start.9 = (bf16[2048]{0:T(1024)(128)(2,1)S(1)}, bf16[2048]{0:T(1024)(128)(2,1)}, u32[]{:S(2)}) copy-start(bf16[2048]{0:T(1024)(128)(2,1)} %param.20) | copy-start | bytes 12292
  15.6 145.5 %all-to-all-start = ((bf16[4,16,48,2048]{3,2,1,0:T(8,128)(2,1)}), bf16[4,16,48,2048]{3,2,1,0:T(8,128)(2,1)}, u32[]{:S(2)}, u32[]{:S(2)}) async-start(bf16[4,16,48,2048]{3,2,1,0:T(8,128)(2,1)} %bitcast.100), calls=%async_computation | async-start | bytes 25165824 | tf_op jit(solution)/shard_map/all_to_all | solution.py:93
  297.6 6.7 %copy-start.1 = (bf16[1,256,2048]{2,1,0:T(8,128)(2,1)S(1)}, bf16[1,256,2048]{2,1,0:T(8,128)(2,1)}, u32[]{:S(2)}) copy-start(bf16[1,256,2048]{2,1,0:T(8,128)(2,1)} %param.17) | copy-start | bytes 3145732
  297.6 144.4 %all-to-all-start.1 = ((bf16[4,16,48,2048]{3,2,1,0:T(8,128)(2,1)}), bf16[4,16,48,2048]{3,2,1,0:T(8,128)(2,1)}, u32[]{:S(2)}, u32[]{:S(2)}) async-start(bf16[4,16,48,2048]{3,2,1,0:T(8,128)(2,1)} %copy.59), calls=%async_computation.1 | async-start | bytes 25165824 | tf_op jit(solution)/shard_map/all_to_all | solution.py:95
  322.9 12.3 %copy-start.10 = (bf16[2048]{0:T(1024)(128)(2,1)S(1)}, bf16[2048]{0:T(1024)(128)(2,1)}, u32[]{:S(2)}) copy-start(bf16[2048]{0:T(1024)(128)(2,1)} %param.25) | copy-start | bytes 12292
  322.9 12.3 %copy-start.6 = (f32[2048]{0:T(1024)S(1)}, f32[2048]{0:T(1024)}, u32[]{:S(2)}) copy-start(f32[2048]{0:T(1024)} %copy-done.5) | copy-start | bytes 24580
  322.9 12.8 %copy-start.7 = (s32[1,256,6]{1,2,0:T(8,128)S(1)}, s32[1,256,6]{1,2,0:T(8,128)}, u32[]{:S(2)}) copy-start(s32[1,256,6]{1,2,0:T(8,128)} %copy.79) | copy-start | bytes 18436
  349.4 2.3 slice-start
  351.1 2.3 slice-start.1
  351.1 9.0 %slice-start.2 = ((s8[11534336]{0:T(1024)(128)(4,1)}), s8[4194304]{0:T(1024)(128)(4,1)S(1)}, s32[]{:S(2)}) async-start(s8[11534336]{0:T(1024)(128)(4,1)} %bitcast.110), calls=%async_computation.4 | async-start | bytes 8388608
  351.1 9.0 %slice-start.3 = ((s8[11534336]{0:T(1024)(128)(4,1)}), s8[4194304]{0:T(1024)(128)(4,1)S(1)}, s32[]{:S(2)}) async-start(s8[11534336]{0:T(1024)(128)(4,1)} %bitcast.110), calls=%async_computation.5 | async-start | bytes 8388608
  353.4 2.5 copy-start.4
  353.4 6.7 %slice-start.4 = ((s8[11534336]{0:T(1024)(128)(4,1)}), s8[3145728]{0:T(1024)(128)(4,1)S(1)}, s32[]{:S(2)}) async-start(s8[11534336]{0:T(1024)(128)(4,1)} %bitcast.110), calls=%async_computation.6 | async-start | bytes 6291456
  355.9 4.2 copy-start.2
  448.4 6.6 %copy-start.11 = (f32[1,256,2048]{2,1,0:T(8,128)S(1)}, f32[1,256,2048]{2,1,0:T(8,128)}, u32[]{:S(2)}) copy-start(f32[1,256,2048]{2,1,0:T(8,128)} %convert_add_fusion) | copy-start | bytes 6291460
where the time goes:
time: 471 us; the launch traced here: 464 us
  matrix products  199 us (42%)
  waiting for transfers between devices  198 us (42%)
  local copies, waits for them, and re-layouts  38.9 us (8%)
  other arithmetic  14.1 us (3%)
  starting transfers between devices  13.3 us (3%)
    dot_general x16, matrix products, _mm(): return jnp.einsum(form, a, b, preferred_element_type=jnp.float32)  199 us
    all_to_all x1, waiting for transfers between devices, local(): recv = lax.all_to_all(send, 'ep', 0, 0, tiled=True)  138 us
    all_to_all x1, waiting for transfers between devices, local(): back = lax.all_to_all(y, 'ep', 0, 0, tiled=True).reshape(ne * cap, d)  60.1 us
    dot_general x2, local copies, waits for them, and re-layouts, _mm(): return jnp.einsum(form, a, b, preferred_element_type=jnp.float32)  24.7 us
    convert_element_type x1, local copies, waits for them, and re-layouts, _experts(): return _mm('egcf,efd->gecd', he, ue2).astype(jnp.bfloat16)  10.7 us
  transfers between devices with their start and end apart: 2, of which 2 were waited for; matrix products, arithmetic and copies ran while one was open for 16% of the time, Pallas kernels for 0%

commit v1 on v0

v1 whole, which is shorter than its diff:
```python
import jax
import jax.numpy as jnp
import numpy as np
from jax import lax
from jax.experimental import pallas as pl
from jax.experimental.pallas import tpu as pltpu
from jax.sharding import PartitionSpec as P

MESH = pl.DeviceIdType.MESH
F32 = jnp.float32
BF16 = jnp.bfloat16
EPS = 1e-6
HEAD = 128
CAP_FACTOR = 2

OWN, SIB, CROSS, DIAG = range(4)
NA = 4
NB = 6
CC = 512
UC = 4


def _dot(a, b):
    return jnp.dot(a, b, preferred_element_type=F32)


def _rope_tables(s):
    half = HEAD // 2
    freq = np.float32(10000.0) ** (-np.arange(half, dtype=np.float32) / np.float32(half))
    ang = np.arange(s, dtype=np.float32)[:, None] * freq.astype(np.float32)[None, :]
    c, sn = np.cos(ang), np.sin(ang)
    return np.concatenate([c, c], 1).astype(np.float32), np.concatenate([-sn, sn], 1).astype(np.float32)


def _build(t, d, fe, fs, el, cap, top):
    nh = d // HEAD
    rows = 4 * cap
    rl = el * cap
    nch = d // CC
    uc = t // UC
    nta = 8 + 2 * el
    nue2 = nch * el
    nf = fs // fe

    def kernel(h0_hbm, idx_ref, slot_ref, ln_ref, cos_ref, sin_ref, wr_ref, wq, wk, wv, wo, ws1, ws3, ws2,
               ue1, ue3, ue2, out_hbm,
               ring_a, ring_b, u_all, xy, he, hsf, h0v, x1v, mrow, mcol,
               macc, rsib, rcross, rdiag, sdiag, ssib,
               sem_a, sem_b, sem_in, sem_out,
               ms, mr, us_sib, ur_sib, us_cross, ur_cross, us_fwd, ur_diag,
               cs_diag, cr_diag, cs_sib, cr_sib, cs_cross, cr_cross):
        me = lax.axis_index('ep')
        core = lax.rem(me, 2)
        sib = me + 1 - 2 * core
        cross = lax.rem(me + 2, 4)
        diag = lax.rem(sib + 2, 4)
        base = (me * rl).astype(F32)

        def rcopy(src, dst, ssem, rsem, dev):
            return pltpu.make_async_remote_copy(src_ref=src, dst_ref=dst, send_sem=ssem, recv_sem=rsem,
                                                device_id={'ep': dev}, device_id_type=MESH)

        def a_dense(k):
            w = (wq, wk, wv, wo)[k // 2]
            return pltpu.make_async_copy(w.at[:, pl.ds((k % 2) * (d // 2), d // 2)],
                                         ring_a.at[k % NA, :, pl.ds(0, d // 2)], sem_a.at[k % NA])

        def a_expert(e, s):
            return pltpu.make_async_copy((ue1, ue3)[s % 2].at[e], ring_a.at[s], sem_a.at[s])

        def a_shared(k):
            return pltpu.make_async_copy((ws1, ws3)[k % 2].at[:, pl.ds((k // 2) * fe, fe)],
                                         ring_a.at[k], sem_a.at[k])

        def b_ue2(i):
            sl = lax.rem(i, NB)
            return pltpu.make_async_copy(
                ue2.at[lax.rem(i, el), :, pl.ds(pl.multiple_of(lax.div(i, el) * CC, CC), CC)],
                ring_b.at[sl], sem_b.at[sl])

        def b_ws2(i):
            k = i - nue2
            sl = lax.rem(i, NB)
            return pltpu.make_async_copy(
                ws2.at[pl.ds(pl.multiple_of(lax.rem(k, nf) * fe, 128), fe),
                       pl.ds(pl.multiple_of(lax.div(k, nf) * CC, CC), CC)],
                ring_b.at[sl], sem_b.at[sl])

        h0_in = pltpu.make_async_copy(h0_hbm, h0v, sem_in)
        h0_in.start()
        for k in range(NA):
            a_dense(k).start()
        bar = pltpu.get_barrier_semaphore()
        for dev in (sib, cross, diag):
            pl.semaphore_signal(bar, inc=1, device_id={'ep': dev}, device_id_type=MESH)
        pl.semaphore_wait(bar, 3)
        h0_in.wait()

        def u_sib(i):
            r = pl.ds(i * uc, uc)
            return rcopy(u_all.at[OWN, r, pl.ds(0, d)], u_all.at[SIB, r, pl.ds(0, d)], us_sib.at[i], ur_sib.at[i], sib)

        def u_cross(i):
            r = pl.ds(i * uc, uc)
            return rcopy(u_all.at[OWN, r, pl.ds(0, d)], u_all.at[CROSS, r, pl.ds(0, d)],
                         us_cross.at[i], ur_cross.at[i], cross)

        def u_fwd(i):
            r = pl.ds(i * uc, uc)
            return rcopy(u_all.at[CROSS, r, pl.ds(0, d)], u_all.at[DIAG, r, pl.ds(0, d)],
                         us_fwd.at[i], ur_diag.at[i], sib)

        def relay(i):
            u_cross(i).wait_recv()
            u_fwd(i).start()

        for i in range(UC):
            def norm_in(k, _):
                r = pl.ds(pl.multiple_of(i * uc + k * 16, 16), 16)
                x = h0v[r, :].astype(F32)
                n = x * lax.rsqrt(jnp.mean(x * x, axis=-1, keepdims=True) + EPS)
                u_all[OWN, r, 0:d] = (n * ln_ref[2:3, :]).astype(BF16)
                x1v[r, :] = (n * ln_ref[0:1, :]).astype(BF16)
                return 0

            lax.fori_loop(0, uc // 16, norm_in, 0)
            u_cross(i).start()
            u_sib(i).start()

        lg = _dot(u_all[OWN, :, 0:d], wr_ref[...])
        ex = lax.broadcasted_iota(jnp.int32, lg.shape, 1)
        lj = [jnp.sum(jnp.where(ex == idx_ref[:, j:j + 1], lg, 0.0), axis=-1, keepdims=True) for j in range(top)]
        mx = lj[0]
        for j in range(1, top):
            mx = jnp.maximum(mx, lj[j])
        ej = [jnp.exp(v - mx) for v in lj]
        tot = ej[0]
        for j in range(1, top):
            tot = tot + ej[j]
        lane = lax.broadcasted_iota(jnp.int32, (t, 128), 1)
        meta = jnp.zeros((t, 128), F32)
        for j in range(top):
            pos = (idx_ref[:, j:j + 1] * cap + slot_ref[:, j:j + 1]).astype(F32)
            meta = jnp.where(lane == j, pos, meta)
            meta = jnp.where(lane == 8 + j, ej[j] / tot, meta)
        mcol[OWN] = meta
        mrow[OWN] = jnp.transpose(meta)[0:16, :]
        m_copies = [rcopy(mrow.at[OWN], mrow.at[role], ms.at[role - 1], mr.at[role - 1], dev)
                    for role, dev in ((SIB, sib), (CROSS, cross), (DIAG, diag))]
        for c in m_copies:
            c.start()

        def qkv(k, rope):
            a_dense(k).wait()

            def half(n, _):
                y = _dot(x1v[...], ring_a[k % NA, :, pl.ds(pl.multiple_of(n * 512, 512), 512)])
                for h in range(4):
                    yh = y[:, h * HEAD:(h + 1) * HEAD]
                    if rope:
                        yh = yh * cos_ref[...] + pltpu.roll(yh, HEAD // 2, 1) * sin_ref[...]
                    col = pl.multiple_of(n * 512 + ((k % 2) * (d // 2) + h * HEAD), HEAD)
                    xy[(k // 2) * t:(k // 2 + 1) * t, pl.ds(col, HEAD)] = yh.astype(BF16)
                return 0

            lax.fori_loop(0, 2, half, 0)

        for k in range(6):
            qkv(k, k < 4)
            if k < 4:
                a_dense(k + NA).start()
            else:
                a_expert(0, k % NA - 0).start()
        relay(0)
        for i in range(NB):
            b_ue2(i).start()

        ri = lax.broadcasted_iota(jnp.int32, (t, t), 0)
        ci = lax.broadcasted_iota(jnp.int32, (t, t), 1)

        def head_pair(hp, _):
            for s in range(2):
                col = pl.ds(pl.multiple_of((hp * 2 + s) * HEAD, HEAD), HEAD)
                q = xy[0:t, col]
                kk = xy[t:2 * t, col]
                vv = xy[2 * t:3 * t, col]
                sc = lax.dot_general(q, kk, (((1,), (1,)), ((), ())), preferred_element_type=F32) * HEAD ** -0.5
                sc = jnp.where(ri >= ci, sc, -1e30)
                p = jnp.exp(sc - jnp.max(sc, axis=-1, keepdims=True))
                p = (p / jnp.sum(p, axis=-1, keepdims=True)).astype(BF16)
                xy[0:t, col] = _dot(p, vv).astype(BF16)
            return 0

        lax.fori_loop(0, nh // 2, head_pair, 0)
        relay(1)

        for k in (6, 7):
            a_dense(k).wait()

            def half(n, _):
                col = pl.ds(pl.multiple_of((k % 2) * (d // 2) + n * 512, 512), 512)
                y = _dot(xy[0:t, :], ring_a[k % NA, :, pl.ds(pl.multiple_of(n * 512, 512), 512)])
                h0v[:, col] = (h0v[:, col].astype(F32) + y).astype(BF16)
                return 0

            lax.fori_loop(0, 2, half, 0)
            a_expert(1, k % NA).start()

        def norm_a(k, _):
            r = pl.ds(pl.multiple_of(k * 16, 16), 16)
            x = h0v[r, :].astype(F32)
            n = x * lax.rsqrt(jnp.mean(x * x, axis=-1, keepdims=True) + EPS)
            x1v[r, :] = (n * ln_ref[1:2, :]).astype(BF16)
            return 0

        lax.fori_loop(0, t // 16, norm_a, 0)

        for c in m_copies:
            c.wait()
        for role in (SIB, CROSS, DIAG):
            mcol[role] = jnp.transpose(jnp.concatenate([mrow[role], jnp.zeros((112, t), F32)], axis=0))
        for i in range(2, UC):
            relay(i)
        for i in range(UC):
            u_sib(i).wait()
            u_cross(i).wait_send()
            u_fwd(i).wait()

        def group(g, _):
            def gather(role, _):
                rr = (lax.broadcasted_iota(jnp.int32, (rows, t), 0) + g * rows).astype(F32) + base
                hit = rr == mrow[role, 0:1, :]
                for j in range(1, top):
                    hit = hit | (rr == mrow[role, j:j + 1, :])
                oh = jnp.where(hit, 1.0, 0.0).astype(BF16)
                for n in range(d // 512):
                    xg = _dot(oh, u_all[role, :, n * 512:(n + 1) * 512]).astype(BF16)
                    for e4 in range(4):
                        xy[pl.ds(pl.multiple_of(e4 * rows + role * cap, 16), cap), n * 512:(n + 1) * 512] = (
                            xg[e4 * cap:(e4 + 1) * cap, :])
                return 0

            lax.fori_loop(0, 4, gather, 0)

            def pair(pp, _):
                e0 = g * 4 + pp * 2
                for s in range(2):
                    e = e0 + s
                    xr = pl.ds(pl.multiple_of((pp * 2 + s) * rows, 16), rows)
                    hr = pl.ds(pl.multiple_of(e * rows, 16), rows)
                    for w in range(2):
                        sl = 2 * s + w
                        a_expert(e, sl).wait()
                        for n0 in range(0, fe, 512):
                            n1 = min(n0 + 512, fe)
                            y = _dot(xy[xr, :], ring_a[sl, :, n0:n1])
                            if w == 0:
                                hsf[0:rows, n0:n1] = y * jax.nn.sigmoid(y)
                            else:
                                he[hr, n0:n1] = (hsf[0:rows, n0:n1] * y).astype(BF16)

                        @pl.when(e0 + 2 < el)
                        def _():
                            a_expert(e + 2, sl).start()

                        @pl.when(e0 + 2 >= el)
                        def _():
                            a_shared(sl).start()
                return 0

            lax.fori_loop(0, 2, pair, 0)
            return 0

        lax.fori_loop(0, el // 4, group, 0)

        def gates(i, _):
            role = lax.div(i, t // 64)
            r = pl.ds(pl.multiple_of(lax.rem(i, t // 64) * 64, 64), 64)
            for b in range(rl // 256):
                rr = (lax.broadcasted_iota(jnp.int32, (64, 256), 1) + b * 256).astype(F32) + base
                comb = jnp.zeros((64, 256), F32)
                for j in range(top):
                    comb = jnp.where(rr == mcol[role, r, j:j + 1], mcol[role, r, 8 + j:9 + j], comb)
                for part in range(3):
                    piece = comb.astype(BF16)
                    u_all[role, r, part * rl + b * 256:part * rl + (b + 1) * 256] = piece
                    comb = comb - piece.astype(F32)
            return 0

        lax.fori_loop(0, 4 * (t // 64), gates, 0)

        def c_diag(c):
            return rcopy(sdiag.at[lax.rem(c, 2)], rdiag.at[c], cs_diag.at[c], cr_diag.at[c], sib)

        def c_sib(c):
            return rcopy(ssib.at[lax.rem(c, 2)], rsib.at[c], cs_sib.at[c], cr_sib.at[c], sib)

        def c_cross(c):
            return rcopy(rdiag.at[c], rcross.at[c], cs_cross.at[c], cr_cross.at[c], cross)

        def partial(role):
            yc = xy[:, role * CC:(role + 1) * CC]
            return (_dot(u_all[role, :, 0:rl], yc) + _dot(u_all[role, :, rl:2 * rl], yc)
                    + _dot(u_all[role, :, 2 * rl:3 * rl], yc))

        def chunk(c, _):
            def four(q, _):
                for s in range(4):
                    e = q * 4 + s
                    i = c * el + e
                    sl = lax.rem(i, NB)
                    b_ue2(i).wait()
                    y = _dot(he[pl.ds(pl.multiple_of(e * rows, 16), rows), :], ring_b[sl]).astype(BF16)
                    for role in range(4):
                        xy[pl.ds(pl.multiple_of(e * cap, 16), cap), role * CC:(role + 1) * CC] = (
                            y[role * cap:(role + 1) * cap, :])

                    @pl.when(i + NB < nue2)
                    def _():
                        b_ue2(i + NB).start()

                    @pl.when(i + NB >= nue2)
                    def _():
                        b_ws2(i + NB).start()
                return 0

            lax.fori_loop(0, el // 4, four, 0)

            @pl.when(c >= 2)
            def _():
                c_diag(c - 2).wait_send()
                c_sib(c - 2).wait_send()

            sdiag[lax.rem(c, 2)] = partial(DIAG)
            c_diag(c).start()
            ssib[lax.rem(c, 2)] = partial(SIB)
            c_sib(c).start()
            macc[c] = partial(OWN)
            pc = partial(CROSS)
            c_diag(c).wait_recv()
            rdiag[c] = rdiag[c] + pc
            c_cross(c).start()
            return 0

        lax.fori_loop(0, nch, chunk, 0)

        for half in range(nf):
            for w in range(2):
                k = half * 2 + w
                a_shared(k).wait()

                def cols_of(n, width):
                    cols = pl.ds(n, width)
                    y = _dot(x1v[...], ring_a[k, :, cols])
                    if w == 0:
                        hsf[:, cols] = y * jax.nn.sigmoid(y)
                    else:
                        he[half * t:(half + 1) * t, cols] = (hsf[:, cols] * y).astype(BF16)

                def step(n, _):
                    cols_of(pl.multiple_of(n * 512, 512), 512)
                    return 0

                lax.fori_loop(0, fe // 512, step, 0)
                if fe % 512:
                    cols_of(fe - fe % 512, fe % 512)

        def shared_out(c, _):
            for half in range(nf):
                i = nue2 + c * nf + half
                b_ws2(i).wait()
                macc[c] += _dot(he[half * t:(half + 1) * t, :], ring_b[lax.rem(i, NB)])

                @pl.when(i + NB < nue2 + nf * nch)
                def _():
                    b_ws2(i + NB).start()
            return 0

        lax.fori_loop(0, nch, shared_out, 0)
        for c in range(nch):
            cols = slice(c * CC, (c + 1) * CC)
            c_sib(c).wait_recv()
            c_cross(c).wait_recv()

            def fin(k, _):
                r = pl.ds(pl.multiple_of(k * 32, 32), 32)
                x1v[r, cols] = (h0v[r, cols].astype(F32) + macc[c, r] + (rsib[c, r] + rcross[c, r])).astype(BF16)
                return 0

            lax.fori_loop(0, t // 32, fin, 0)
            pltpu.make_async_copy(x1v.at[:, pl.ds(c * CC, CC)], out_hbm.at[:, pl.ds(c * CC, CC)],
                                  sem_out.at[c]).start()
        for c in range(nch):
            if c >= nch - 2:
                c_diag(c).wait_send()
                c_sib(c).wait_send()
            c_cross(c).wait_send()
            pltpu.make_async_copy(x1v.at[:, pl.ds(c * CC, CC)], out_hbm.at[:, pl.ds(c * CC, CC)],
                                  sem_out.at[c]).wait()

    dma = pltpu.SemaphoreType.DMA
    vm = pltpu.VMEM
    any_ = pl.BlockSpec(memory_space=pl.ANY)
    vmem = pl.BlockSpec(memory_space=pltpu.VMEM)
    return pl.pallas_call(
        kernel,
        out_shape=jax.ShapeDtypeStruct((t, d), BF16),
        in_specs=[any_] + [vmem] * 6 + [any_] * 10,
        out_specs=any_,
        scratch_shapes=[
            vm((NA, d, fe), BF16),
            vm((NB, fe, CC), BF16),
            vm((4, t, max(d, 3 * rl)), BF16),
            vm((max(4 * rows, 3 * t, rl), d), BF16),
            vm((el * rows, fe), BF16),
            vm((t, fe), F32),
            vm((t, d), BF16),
            vm((t, d), BF16),
            vm((4, 16, t), F32),
            vm((4, t, 128), F32),
            vm((nch, t, CC), F32),
            vm((nch, t, CC), F32),
            vm((nch, t, CC), F32),
            vm((nch, t, CC), F32),
            vm((2, t, CC), F32),
            vm((2, t, CC), F32),
            dma((NA,)), dma((NB,)), dma, dma((nch,)),
            dma((3,)), dma((3,)),
            dma((UC,)), dma((UC,)), dma((UC,)), dma((UC,)), dma((UC,)), dma((UC,)),
            dma((nch,)), dma((nch,)), dma((nch,)), dma((nch,)), dma((nch,)), dma((nch,)),
        ],
        compiler_params=pltpu.CompilerParams(collective_id=0, has_side_effects=True,
                                             vmem_limit_bytes=67043328),
        name='moe_layer',
    )


def solution(mesh):
    g_ = mesh.shape['ep']
    rows = P(('dp', 'ep'))
    rep = P()

    def local(h0, idx, slot, ln_attn, wq, wk, wv, wo, ln_ffn, ws1, ws3, ws2, ln_moe, wr, ue1, ue3, ue2):
        b, s, d = h0.shape
        top = idx.shape[-1]
        el, _, fe = ue1.shape
        t = b * s
        cap = CAP_FACTOR * t * top // (el * g_)
        lns = jnp.stack([ln_attn, ln_ffn, ln_moe]).astype(F32)
        cos, sin = _rope_tables(s)
        call = _build(t, d, fe, ws1.shape[1], el, cap, top)
        out = call(h0.reshape(t, d), idx.reshape(t, top), slot.reshape(t, top), lns, cos, sin, wr,
                   wq, wk, wv, wo, ws1, ws3, ws2, ue1, ue3, ue2)
        return out.reshape(b, s, d)

    specs = (rows, rows, rows) + (rep,) * 11 + (P('ep'), P('ep'), P('ep'))
    return jax.shard_map(local, mesh=mesh, in_specs=specs, out_specs=rows, check_vma=False)
```

time: 471 us -> 168 us (0.36); the launches traced: 464 us -> 167 us
  matrix products: 199 us -> 0 us
  waiting for transfers between devices: 198 us -> 0 us
  Pallas kernels: 0 us -> 157 us
  local copies, waits for them, and re-layouts: 38.9 us -> 9.29 us
  other arithmetic: 14.1 us -> 0.63 us
  starting transfers between devices: 13.3 us -> 0 us
    dot_general x16 -> x0, matrix products: 199 us -> none  [_mm(): return jnp.einsum(form, a, b, preferred_element_type=jnp.float32)]
    all_to_all x2 -> x0, waiting for transfers between devices: 198 us -> none  [the longest x1 138 us: local(): recv = lax.all_to_all(send, 'ep', 0, 0, tiled=True)]
    pallas_call x0 -> x1, Pallas kernels: none -> 157 us  [local(): call(h0.reshape(t, d), idx.reshape(t, top), slot.reshape(t, top), lns, co...]
    dot_general x2 -> x0, local copies, waits for them, and re-layouts: 24.7 us -> none  [_mm(): return jnp.einsum(form, a, b, preferred_element_type=jnp.float32)]
    all_to_all x2 -> x0, starting transfers between devices: 13.3 us -> none  [the longest x1 6.66 us: local(): back = lax.all_to_all(y, 'ep', 0, 0, tiled=True).reshape(ne * cap, d)]
    convert_element_type x1 -> x0, local copies, waits for them, and re-layouts: 10.7 us -> none  [_experts(): return _mm('egcf,efd->gecd', he, ue2).astype(jnp.bfloat16)]
    reduce_sum x4 -> x0, other arithmetic: 5.78 us -> none  [the longest x1 4.15 us: _route(): comb = jnp.sum(jnp.where(hit, gate[..., None], 0.0), axis=-2)]
  transfers between devices with their start and end apart: 2 -> 0, of which waited for: 2 -> 0; matrix products, arithmetic and copies ran while one was open for 16% -> 0% of each run, Pallas kernels for 0% -> 0%
where the time goes in v1:
time: 168 us; the launch traced here: 167 us
  Pallas kernels  157 us (93%)
  local copies, waits for them, and re-layouts  9.29 us (6%)
    pallas_call x1, Pallas kernels, local(): call(h0.reshape(t, d), idx.reshape(t, top), slot.reshape(t, top), lns, co...  157 us
    unnamed x4, local copies, waits for them, and re-layouts  7.21 us

profile of v1, /device:TPU:0, one launch (start us, length us, event | category | flops | bytes accessed | tf_op | source)
XLA Modules:
  0.0 167.4 jit_solution(16181274235129037567)
XLA Ops:
  0.0 0.7 stack.12
  0.7 0.7 stack.13
  1.4 0.7 stack.14
  2.1 0.6 maximum_convert_fusion.ln_ref
  2.7 1.5 copy.20
  4.2 1.5 copy.21
  5.7 2.0 %copy.22.wr_ref = bf16[2048,64]{1,0:T(8,128)(2,1)} copy(bf16[2048,64]{0,1:T(8,128)(2,1)} %param.32) | data formatting | bytes 524288 | tf_op args[13]
  7.6 157.5 %moe_layer.1 = bf16[256,2048]{1,0:T(8,128)(2,1)} custom-call(bf16[256,2048]{1,0:T(8,128)(2,1)} %bitcast.5, s32[256,6]{1,0:T(8,128)} %bitcast.6, s32[256,6]{1,0:T(8,128)} %bitcast.7, f32[3,2048]{1,0:T(4,128)} %maximum_convert_fusion.ln_ref, f32[256,128]{1,0:T(8,128)} %constant.4.clone.cos_ref, f32[256,128]{1,0:T(8,128)} %constant.5.clone.sin_ref, ...), custom_call_target="tpu_custom_call" | custom-call | tf_op jit(solution)/shard_map/moe_layer/pallas_call | solution.py:452
  165.1 2.3 %copy.24 = bf16[1,256,2048]{2,1,0:T(8,128)(2,1)} copy(bf16[1,256,2048]{2,1,0:T(8,128)(2,1)} %bitcast.4) | data formatting | bytes 2097152

commit v2 on v1

v2 whole, which is shorter than its diff:
```python
import jax
import jax.numpy as jnp
import numpy as np
from jax import lax
from jax.experimental import pallas as pl
from jax.experimental.pallas import tpu as pltpu
from jax.sharding import PartitionSpec as P

MESH = pl.DeviceIdType.MESH
F32 = jnp.float32
BF16 = jnp.bfloat16
EPS = 1e-6
HEAD = 128
CAP_FACTOR = 2

OWN, SIB, CROSS, DIAG = range(4)
NA = 4
NB = 3
EB = 4
CC = 256
UC = 8


def _dot(a, b):
    return jnp.dot(a, b, preferred_element_type=F32)


def _rope_tables(s):
    half = HEAD // 2
    freq = np.float32(10000.0) ** (-np.arange(half, dtype=np.float32) / np.float32(half))
    ang = np.arange(s, dtype=np.float32)[:, None] * freq.astype(np.float32)[None, :]
    c, sn = np.cos(ang), np.sin(ang)
    return np.concatenate([c, c], 1).astype(np.float32), np.concatenate([-sn, sn], 1).astype(np.float32)


def _build(t, d, fe, fs, el, cap, top):
    nh = d // HEAD
    rows = 4 * cap
    rl = el * cap
    nch = d // CC
    uc = t // UC
    nta = 8 + 2 * el
    nue2 = nch * el // EB
    nf = fs // fe
    cpt = EB // nf
    nws2 = nch // cpt

    def kernel(h0_hbm, idx_ref, slot_ref, lna_ref, lnf_ref, lnm_ref, cos_ref, sin_ref, wr_ref, wq, wk, wv, wo, ws1, ws3, ws2,
               ue1, ue3, ue2, out_hbm,
               ring_a, ring_b, u_all, comb, xy, he, ln_ref, h0v, x1v, mrow, mcol,
               macc, rsib, rcross, rdiag, sdiag, ssib,
               sem_a, sem_b, sem_in, sem_out,
               ms, mr, us_sib, ur_sib, us_cross, ur_cross, us_fwd, ur_diag,
               cs_diag, cr_diag, cs_sib, cr_sib, cs_cross, cr_cross):
        me = lax.axis_index('ep')
        core = lax.rem(me, 2)
        sib = me + 1 - 2 * core
        cross = lax.rem(me + 2, 4)
        diag = lax.rem(sib + 2, 4)
        base = (me * rl).astype(F32)

        def rcopy(src, dst, ssem, rsem, dev):
            return pltpu.make_async_remote_copy(src_ref=src, dst_ref=dst, send_sem=ssem, recv_sem=rsem,
                                                device_id={'ep': dev}, device_id_type=MESH)

        def a_dense(k):
            w = (wq, wk, wv, wo)[k // 2]
            return pltpu.make_async_copy(w.at[:, pl.ds((k % 2) * (d // 2), d // 2)],
                                         ring_a.at[k % NA, :, pl.ds(0, d // 2)], sem_a.at[k % NA])

        def a_expert(e, s):
            return pltpu.make_async_copy((ue1, ue3)[s % 2].at[e], ring_a.at[s], sem_a.at[s])

        def a_shared(k):
            return pltpu.make_async_copy((ws1, ws3)[k % 2].at[:, pl.ds((k // 2) * fe, fe)],
                                         ring_a.at[k], sem_a.at[k])

        def b_ue2(i):
            sl = lax.rem(i, NB)
            e0 = lax.rem(i, el // EB) * EB
            col = pl.multiple_of(lax.div(i, el // EB) * CC, CC)
            return pltpu.make_async_copy(ue2.at[pl.ds(e0, EB), :, pl.ds(col, CC)], ring_b.at[sl], sem_b.at[sl, 0])

        def b_ws2(i):
            sl = lax.rem(i, NB)
            k = i - nue2
            return [pltpu.make_async_copy(
                ws2.at[pl.ds(half * fe, fe), pl.ds(pl.multiple_of((k * cpt + u) * CC, CC), CC)],
                ring_b.at[sl, u * nf + half], sem_b.at[sl, u * nf + half])
                for u in range(cpt) for half in range(nf)]

        h0_in = pltpu.make_async_copy(h0_hbm, h0v, sem_in)
        h0_in.start()
        bar = pltpu.get_barrier_semaphore()
        for dev in (sib, cross, diag):
            pl.semaphore_signal(bar, inc=1, device_id={'ep': dev}, device_id_type=MESH)
        for k, ref in enumerate((lna_ref, lnf_ref, lnm_ref)):
            w = ref[...].astype(F32)
            for i in range(d // 128):
                ln_ref[k:k + 1, i * 128:(i + 1) * 128] = w[i:i + 1, :]
        h0_in.wait()
        for k in range(NA):
            a_dense(k).start()

        def u_sib(i):
            r = pl.ds(i * uc, uc)
            return rcopy(u_all.at[OWN, r], u_all.at[SIB, r], us_sib.at[i], ur_sib.at[i], sib)

        def u_cross(i):
            r = pl.ds(i * uc, uc)
            return rcopy(u_all.at[OWN, r], u_all.at[CROSS, r],
                         us_cross.at[i], ur_cross.at[i], cross)

        def u_fwd(i):
            r = pl.ds(i * uc, uc)
            return rcopy(u_all.at[CROSS, r], u_all.at[DIAG, r],
                         us_fwd.at[i], ur_diag.at[i], sib)

        def relay(i):
            u_cross(i).wait_recv()
            u_fwd(i).start()

        def norm_in(k, _):
            r = pl.ds(pl.multiple_of(k * 16, 16), 16)
            x = h0v[r, :].astype(F32)
            n = x * lax.rsqrt(jnp.mean(x * x, axis=-1, keepdims=True) + EPS)
            u_all[OWN, r, :] = (n * ln_ref[2:3, :]).astype(BF16)
            x1v[r, :] = (n * ln_ref[0:1, :]).astype(BF16)
            return 0

        lax.fori_loop(0, t // 32, norm_in, 0)
        pl.semaphore_wait(bar, 3)
        for i in range(UC // 2):
            u_cross(i).start()
            u_sib(i).start()
        lax.fori_loop(t // 32, t // 16, norm_in, 0)

        lg = lax.dot_general(wr_ref[...], u_all[OWN], (((1,), (1,)), ((), ())), preferred_element_type=F32)
        ex = lax.broadcasted_iota(jnp.int32, lg.shape, 0)
        lj = [jnp.sum(jnp.where(ex == idx_ref[j], lg, 0.0), axis=0, keepdims=True) for j in range(top)]
        mx = lj[0]
        for j in range(1, top):
            mx = jnp.maximum(mx, lj[j])
        ej = [jnp.exp(v - mx) for v in lj]
        tot = ej[0]
        for j in range(1, top):
            tot = tot + ej[j]
        mrow[OWN] = jnp.zeros((16, t), F32)
        for j in range(top):
            mrow[OWN, j:j + 1, :] = (idx_ref[j] * cap + slot_ref[j]).astype(F32)
            mrow[OWN, 8 + j:9 + j, :] = ej[j] / tot
        m_copies = [rcopy(mrow.at[OWN], mrow.at[role], ms.at[role - 1], mr.at[role - 1], dev)
                    for role, dev in ((SIB, sib), (CROSS, cross), (DIAG, diag))]
        for c in m_copies:
            c.start()
        for i in range(UC // 2, UC):
            u_cross(i).start()
            u_sib(i).start()

        def qkv(k, rope):
            a_dense(k).wait()

            for n in range(2):
                y = _dot(x1v[...], ring_a[k % NA, :, n * 512:(n + 1) * 512])
                for h in range(4):
                    yh = y[:, h * HEAD:(h + 1) * HEAD]
                    if rope:
                        yh = yh * cos_ref[...] + pltpu.roll(yh, HEAD // 2, 1) * sin_ref[...]
                    col = (k % 2) * (d // 2) + n * 512 + h * HEAD
                    xy[(k // 2) * t:(k // 2 + 1) * t, col:col + HEAD] = yh.astype(BF16)

        for k in range(6):
            qkv(k, k < 4)
            if k < 4:
                a_dense(k + NA).start()
            else:
                a_expert(0, k % NA - 0).start()
        for i in range(2):
            relay(i)
        for i in range(NB):
            b_ue2(i).start()

        ri = lax.broadcasted_iota(jnp.int32, (t, t), 0)
        ci = lax.broadcasted_iota(jnp.int32, (t, t), 1)

        def head_pair(hp, _):
            for s in range(2):
                col = pl.ds(pl.multiple_of((hp * 2 + s) * HEAD, HEAD), HEAD)
                q = xy[0:t, col]
                kk = xy[t:2 * t, col]
                vv = xy[2 * t:3 * t, col]
                sc = lax.dot_general(q, kk, (((1,), (1,)), ((), ())), preferred_element_type=F32) * HEAD ** -0.5
                sc = jnp.where(ri >= ci, sc, -1e30)
                p = jnp.exp(sc - jnp.max(sc, axis=-1, keepdims=True))
                p = (p / jnp.sum(p, axis=-1, keepdims=True)).astype(BF16)
                xy[0:t, col] = _dot(p, vv).astype(BF16)
            return 0

        lax.fori_loop(0, nh // 2, head_pair, 0)
        for i in range(2, 5):
            relay(i)

        for k in (6, 7):
            a_dense(k).wait()

            for n in range(2):
                col = slice((k % 2) * (d // 2) + n * 512, (k % 2) * (d // 2) + (n + 1) * 512)
                y = _dot(xy[0:t, :], ring_a[k % NA, :, n * 512:(n + 1) * 512])
                h0v[:, col] = (h0v[:, col].astype(F32) + y).astype(BF16)
            a_expert(1, k % NA).start()

        def norm_a(k, _):
            r = pl.ds(pl.multiple_of(k * 16, 16), 16)
            x = h0v[r, :].astype(F32)
            n = x * lax.rsqrt(jnp.mean(x * x, axis=-1, keepdims=True) + EPS)
            x1v[r, :] = (n * ln_ref[1:2, :]).astype(BF16)
            return 0

        lax.fori_loop(0, t // 16, norm_a, 0)

        for c in m_copies:
            c.wait()
        for role in range(4):
            mcol[role] = jnp.transpose(jnp.concatenate([mrow[role], jnp.zeros((112, t), F32)], axis=0))
        for i in range(5, UC):
            relay(i)
        for i in range(UC):
            u_sib(i).wait()
            u_cross(i).wait_send()
            u_fwd(i).wait()

        def swiglu(src, sr, sl, dst, dr):
            for n0 in range(0, fe - fe % 256, 256):
                cols = slice(n0, n0 + 256)
                y1 = _dot(src[sr, :], ring_a[sl, :, cols])
                y3 = _dot(src[sr, :], ring_a[sl + 1, :, cols])
                dst[dr, cols] = (y1 * jax.nn.sigmoid(y1) * y3).astype(BF16)
            if fe % 256:
                cols = slice(fe - fe % 256, fe)
                y = _dot(src[sr, :], jnp.concatenate([ring_a[sl, :, cols], ring_a[sl + 1, :, cols]], axis=1))
                y1, y3 = y[:, :fe % 256], y[:, fe % 256:]
                dst[dr, cols] = (y1 * jax.nn.sigmoid(y1) * y3).astype(BF16)

        npart = 4 * t // el
        def gate_part(i):
            role = lax.div(i, el // 4)
            r = pl.ds(pl.multiple_of(lax.rem(i, el // 4) * npart, npart), npart)
            for b in range(rl // 256):
                rr = (lax.broadcasted_iota(jnp.int32, (npart, 256), 1) + b * 256).astype(F32) + base
                w = jnp.zeros((npart, 256), F32)
                for j in range(top):
                    w = jnp.where(rr == mcol[role, r, j:j + 1], mcol[role, r, 8 + j:9 + j], w)
                for part in range(3):
                    piece = w.astype(BF16)
                    comb[role, r, part * rl + b * 256:part * rl + (b + 1) * 256] = piece
                    w = w - piece.astype(F32)

        def group(g, _):
            def gather(role, _):
                rr = (lax.broadcasted_iota(jnp.int32, (rows, t), 0) + g * rows).astype(F32) + base
                hit = rr == mrow[role, 0:1, :]
                for j in range(1, top):
                    hit = hit | (rr == mrow[role, j:j + 1, :])
                oh = jnp.where(hit, 1.0, 0.0).astype(BF16)
                for n in range(d // 512):
                    xg = _dot(oh, u_all[role, :, n * 512:(n + 1) * 512]).astype(BF16)
                    for e4 in range(4):
                        xy[pl.ds(pl.multiple_of(e4 * rows + role * cap, 16), cap), n * 512:(n + 1) * 512] = (
                            xg[e4 * cap:(e4 + 1) * cap, :])
                return 0

            lax.fori_loop(0, 4, gather, 0)

            def pair(pp, _):
                e0 = g * 4 + pp * 2
                for s in range(2):
                    e = e0 + s
                    xr = pl.ds(pl.multiple_of((pp * 2 + s) * rows, 16), rows)
                    hr = pl.ds(pl.multiple_of(e * rows, 16), rows)
                    gate_part(e)
                    a_expert(e, 2 * s).wait()
                    a_expert(e, 2 * s + 1).wait()
                    swiglu(xy, xr, 2 * s, he, hr)

                    @pl.when(e0 + 2 < el)
                    def _():
                        a_expert(e + 2, 2 * s).start()
                        a_expert(e + 2, 2 * s + 1).start()

                    @pl.when(e0 + 2 >= el)
                    def _():
                        a_shared(2 * s).start()
                        a_shared(2 * s + 1).start()
                return 0

            lax.fori_loop(0, 2, pair, 0)
            return 0

        lax.fori_loop(0, el // 4, group, 0)

        def c_diag(c):
            return rcopy(sdiag.at[lax.rem(c, 2)], rdiag.at[c], cs_diag.at[c], cr_diag.at[c], sib)

        def c_sib(c):
            return rcopy(ssib.at[lax.rem(c, 2)], rsib.at[lax.rem(c, 2)], cs_sib.at[c], cr_sib.at[c], sib)

        def c_cross(c):
            return rcopy(rdiag.at[c], rcross.at[c], cs_cross.at[c], cr_cross.at[c], cross)

        def partial(role):
            yc = xy[:, role * CC:(role + 1) * CC]
            return (_dot(comb[role, :, 0:rl], yc) + _dot(comb[role, :, rl:2 * rl], yc)
                    + _dot(comb[role, :, 2 * rl:3 * rl], yc))

        def chunk(c, _):
            def four(q, _):
                i = c * (el // EB) + q
                sl = lax.rem(i, NB)
                b_ue2(i).wait()
                for s in range(EB):
                    e = q * EB + s
                    y = _dot(he[pl.ds(pl.multiple_of(e * rows, 16), rows), :], ring_b[sl, s]).astype(BF16)
                    for role in range(4):
                        xy[pl.ds(pl.multiple_of(e * cap, 16), cap), role * CC:(role + 1) * CC] = (
                            y[role * cap:(role + 1) * cap, :])

                @pl.when(i + NB < nue2)
                def _():
                    b_ue2(i + NB).start()

                @pl.when(i + NB >= nue2)
                def _():
                    for cp in b_ws2(i + NB):
                        cp.start()
                return 0

            lax.fori_loop(0, el // EB, four, 0)

            @pl.when(c >= 2)
            def _():
                c_diag(c - 2).wait_send()
                c_sib(c - 2).wait_send()

            sdiag[lax.rem(c, 2)] = partial(DIAG)
            c_diag(c).start()
            ssib[lax.rem(c, 2)] = partial(SIB)
            c_sib(c).start()
            macc[c] = partial(OWN)
            pc = partial(CROSS)
            c_diag(c).wait_recv()
            rdiag[c] = rdiag[c] + pc
            c_cross(c).start()
            c_sib(c).wait_recv()
            macc[c] = macc[c] + rsib[lax.rem(c, 2)]
            return 0

        lax.fori_loop(0, nch, chunk, 0)

        for half in range(nf):
            a_shared(2 * half).wait()
            a_shared(2 * half + 1).wait()
            swiglu(x1v, slice(0, t), 2 * half, he, slice(half * t, (half + 1) * t))

        def shared_out(k, _):
            i = k + nue2
            for cp in b_ws2(i):
                cp.wait()
            for u in range(cpt):
                f = macc[k * cpt + u]
                for half in range(nf):
                    f = f + _dot(he[half * t:(half + 1) * t, :], ring_b[lax.rem(i, NB), u * nf + half])
                macc[k * cpt + u] = f

            @pl.when(k + NB < nws2)
            def _():
                for cp in b_ws2(i + NB):
                    cp.start()
            return 0

        lax.fori_loop(0, nws2, shared_out, 0)
        for c in range(nch):
            cols = slice(c * CC, (c + 1) * CC)
            c_cross(c).wait_recv()

            def fin(k, _):
                r = pl.ds(pl.multiple_of(k * 32, 32), 32)
                x1v[r, cols] = (h0v[r, cols].astype(F32) + macc[c, r] + rcross[c, r]).astype(BF16)
                return 0

            lax.fori_loop(0, t // 32, fin, 0)
            pltpu.make_async_copy(x1v.at[:, pl.ds(c * CC, CC)], out_hbm.at[:, pl.ds(c * CC, CC)],
                                  sem_out.at[c]).start()
        for c in range(nch):
            if c >= nch - 2:
                c_diag(c).wait_send()
                c_sib(c).wait_send()
            c_cross(c).wait_send()
            pltpu.make_async_copy(x1v.at[:, pl.ds(c * CC, CC)], out_hbm.at[:, pl.ds(c * CC, CC)],
                                  sem_out.at[c]).wait()

    dma = pltpu.SemaphoreType.DMA
    vm = pltpu.VMEM
    any_ = pl.BlockSpec(memory_space=pl.ANY)
    vmem = pl.BlockSpec(memory_space=pltpu.VMEM)
    return pl.pallas_call(
        kernel,
        out_shape=jax.ShapeDtypeStruct((t, d), BF16),
        in_specs=[any_] + [vmem] * 8 + [any_] * 10,
        out_specs=any_,
        scratch_shapes=[
            vm((NA, d, fe), BF16),
            vm((NB, EB, fe, CC), BF16),
            vm((4, t, d), BF16),
            vm((4, t, 3 * rl), BF16),
            vm((max(4 * rows, 3 * t, rl), d), BF16),
            vm((el * rows, fe), BF16),
            vm((8, d), F32),
            vm((t, d), BF16),
            vm((t, d), BF16),
            vm((4, 16, t), F32),
            vm((4, t, 128), F32),
            vm((nch, t, CC), F32),
            vm((2, t, CC), F32),
            vm((nch, t, CC), F32),
            vm((nch, t, CC), F32),
            vm((2, t, CC), F32),
            vm((2, t, CC), F32),
            dma((NA,)), dma((NB, EB)), dma, dma((nch,)),
            dma((3,)), dma((3,)),
            dma((UC,)), dma((UC,)), dma((UC,)), dma((UC,)), dma((UC,)), dma((UC,)),
            dma((nch,)), dma((nch,)), dma((nch,)), dma((nch,)), dma((nch,)), dma((nch,)),
        ],
        compiler_params=pltpu.CompilerParams(collective_id=0, has_side_effects=True,
                                             vmem_limit_bytes=67043328),
        name='moe_layer',
    )


def solution(mesh):
    g_ = mesh.shape['ep']
    rows = P(('dp', 'ep'))
    rep = P()

    def local(h0, idx, slot, ln_attn, wq, wk, wv, wo, ln_ffn, ws1, ws3, ws2, ln_moe, wr, ue1, ue3, ue2):
        b, s, d = h0.shape
        top = idx.shape[-1]
        el, _, fe = ue1.shape
        t = b * s
        cap = CAP_FACTOR * t * top // (el * g_)
        cos, sin = _rope_tables(s)
        gains = [w.reshape(d // 128, 128) for w in (ln_attn, ln_ffn, ln_moe)]
        ids = [jnp.transpose(a, (2, 0, 1)).reshape(top, 1, t) for a in (idx, slot)]
        call = _build(t, d, fe, ws1.shape[1], el, cap, top)
        out = call(h0.reshape(t, d), *ids, *gains, cos, sin, wr.T,
                   wq, wk, wv, wo, ws1, ws3, ws2, ue1, ue3, ue2)
        return out.reshape(b, s, d)

    specs = (rows, rows, rows) + (rep,) * 11 + (P('ep'), P('ep'), P('ep'))
    return jax.shard_map(local, mesh=mesh, in_specs=specs, out_specs=rows, check_vma=False)
```

time: 168 us -> 159 us (0.946)
  local copies, waits for them, and re-layouts: 9.29 us -> 2.3 us
    unnamed x4 -> x1, local copies, waits for them, and re-layouts: 7.21 us -> 2.3 us
    another operation x3 -> x0, local copies, waits for them, and re-layouts: 2.08 us -> none  [local(): lns = jnp.stack([ln_attn, ln_ffn, ln_moe]).astype(F32)]
where the time goes in v2:
time: 159 us
  Pallas kernels  156 us (98%)
  local copies, waits for them, and re-layouts  2.3 us (1%)
    pallas_call x1, Pallas kernels, local(): call(h0.reshape(t, d), *ids, *gains, cos, sin, wr.T, wq, wk, wv, wo, ws1,...  156 us

profile of v2, /device:TPU:0, one launch (start us, length us, event | category | flops | bytes accessed | tf_op | source)
XLA Modules:
  0.0 158.5 jit_solution(6358327739418233524)
XLA Ops:
  0.0 156.2 %moe_layer.1 = bf16[256,2048]{1,0:T(8,128)(2,1)} custom-call(bf16[256,2048]{1,0:T(8,128)(2,1)} %bitcast.9, s32[6,1,256]{2,1,0:T(1,128)} %bitcast.11, s32[6,1,256]{2,1,0:T(1,128)} %bitcast.12, bf16[16,128]{1,0:T(8,128)(2,1)} %bitcast.13, bf16[16,128]{1,0:T(8,128)(2,1)} %bitcast.14, bf16[16,128]{1,0:T(8,128)(2,1)} %bitcast.15, ...), custom_call_target="tpu_custom_call" | custom-call | tf_op jit(solution)/shard_map/moe_layer/pallas_call | solution.py:454
  156.2 2.3 %copy.21 = bf16[1,256,2048]{2,1,0:T(8,128)(2,1)} copy(bf16[1,256,2048]{2,1,0:T(8,128)(2,1)} %bitcast.8) | data formatting | bytes 2097152

commit v3 on v2

--- a/solution.py
+++ b/solution.py
@@ -15,10 +15,11 @@
 
 OWN, SIB, CROSS, DIAG = range(4)
 NA = 4
-NB = 3
+NB = 4
 EB = 4
+ND = 4
 CC = 256
-UC = 8
+UC = 4
 
 
 def _dot(a, b):
@@ -44,10 +45,11 @@
     nf = fs // fe
     cpt = EB // nf
     nws2 = nch // cpt
+    assert el == NB * EB and nws2 == NB
 
     def kernel(h0_hbm, idx_ref, slot_ref, lna_ref, lnf_ref, lnm_ref, cos_ref, sin_ref, wr_ref, wq, wk, wv, wo, ws1, ws3, ws2,
                ue1, ue3, ue2, out_hbm,
-               ring_a, ring_b, u_all, comb, xy, he, ln_ref, h0v, x1v, mrow, mcol,
+               ring_a, ring_b, u_all, comb, xy, he, ln_ref, h0v, x1v, mrow,
                macc, rsib, rcross, rdiag, sdiag, ssib,
                sem_a, sem_b, sem_in, sem_out,
                ms, mr, us_sib, ur_sib, us_cross, ur_cross, us_fwd, ur_diag,
@@ -75,14 +77,12 @@
             return pltpu.make_async_copy((ws1, ws3)[k % 2].at[:, pl.ds((k // 2) * fe, fe)],
                                          ring_a.at[k], sem_a.at[k])
 
-        def b_ue2(i):
-            sl = lax.rem(i, NB)
+        def b_ue2(i, sl):
             e0 = lax.rem(i, el // EB) * EB
             col = pl.multiple_of(lax.div(i, el // EB) * CC, CC)
             return pltpu.make_async_copy(ue2.at[pl.ds(e0, EB), :, pl.ds(col, CC)], ring_b.at[sl], sem_b.at[sl, 0])
 
-        def b_ws2(i):
-            sl = lax.rem(i, NB)
+        def b_ws2(i, sl):
             k = i - nue2
             return [pltpu.make_async_copy(
                 ws2.at[pl.ds(half * fe, fe), pl.ds(pl.multiple_of((k * cpt + u) * CC, CC), CC)],
@@ -175,10 +175,9 @@
                 a_dense(k + NA).start()
             else:
                 a_expert(0, k % NA - 0).start()
-        for i in range(2):
-            relay(i)
+        relay(0)
         for i in range(NB):
-            b_ue2(i).start()
+            b_ue2(i, i).start()
 
         ri = lax.broadcasted_iota(jnp.int32, (t, t), 0)
         ci = lax.broadcasted_iota(jnp.int32, (t, t), 1)
@@ -197,8 +196,7 @@
             return 0
 
         lax.fori_loop(0, nh // 2, head_pair, 0)
-        for i in range(2, 5):
-            relay(i)
+        relay(1)
 
         for k in (6, 7):
             a_dense(k).wait()
@@ -221,25 +219,38 @@
         for c in m_copies:
             c.wait()
         for role in range(4):
-            mcol[role] = jnp.transpose(jnp.concatenate([mrow[role], jnp.zeros((112, t), F32)], axis=0))
-        for i in range(5, UC):
+            macc[role, :, 0:128] = jnp.transpose(jnp.concatenate([mrow[role], jnp.zeros((112, t), F32)], axis=0))
+        for i in range(2, UC):
             relay(i)
         for i in range(UC):
             u_sib(i).wait()
             u_cross(i).wait_send()
             u_fwd(i).wait()
 
-        def swiglu(src, sr, sl, dst, dr):
+        def swiglu(src, sr, sl, dst, dr, between=()):
+            between = list(between)
             for n0 in range(0, fe - fe % 256, 256):
                 cols = slice(n0, n0 + 256)
                 y1 = _dot(src[sr, :], ring_a[sl, :, cols])
                 y3 = _dot(src[sr, :], ring_a[sl + 1, :, cols])
                 dst[dr, cols] = (y1 * jax.nn.sigmoid(y1) * y3).astype(BF16)
+                if between:
+                    between.pop(0)()
             if fe % 256:
                 cols = slice(fe - fe % 256, fe)
                 y = _dot(src[sr, :], jnp.concatenate([ring_a[sl, :, cols], ring_a[sl + 1, :, cols]], axis=1))
                 y1, y3 = y[:, :fe % 256], y[:, fe % 256:]
                 dst[dr, cols] = (y1 * jax.nn.sigmoid(y1) * y3).astype(BF16)
+
+        def gather(e, buf, role):
+            rr = (lax.broadcasted_iota(jnp.int32, (cap, t), 0) + e * cap).astype(F32) + base
+            hit = rr == mrow[role, 0:1, :]
+            for j in range(1, top):
+                hit = hit | (rr == mrow[role, j:j + 1, :])
+            oh = jnp.where(hit, 1.0, 0.0).astype(BF16)
+            r0 = buf * rows + role * cap
+            for n in range(d // 512):
+                xy[r0:r0 + cap, n * 512:(n + 1) * 512] = _dot(oh, u_all[role, :, n * 512:(n + 1) * 512]).astype(BF16)
 
         npart = 4 * t // el
         def gate_part(i):
@@ -249,132 +260,122 @@
                 rr = (lax.broadcasted_iota(jnp.int32, (npart, 256), 1) + b * 256).astype(F32) + base
                 w = jnp.zeros((npart, 256), F32)
                 for j in range(top):
-                    w = jnp.where(rr == mcol[role, r, j:j + 1], mcol[role, r, 8 + j:9 + j], w)
+                    w = jnp.where(rr == macc[role, r, j:j + 1], macc[role, r, 8 + j:9 + j], w)
                 for part in range(3):
                     piece = w.astype(BF16)
                     comb[role, r, part * rl + b * 256:part * rl + (b + 1) * 256] = piece
                     w = w - piece.astype(F32)
 
-        def group(g, _):
-            def gather(role, _):
-                rr = (lax.broadcasted_iota(jnp.int32, (rows, t), 0) + g * rows).astype(F32) + base
-                hit = rr == mrow[role, 0:1, :]
-                for j in range(1, top):
-                    hit = hit | (rr == mrow[role, j:j + 1, :])
-                oh = jnp.where(hit, 1.0, 0.0).astype(BF16)
-                for n in range(d // 512):
-                    xg = _dot(oh, u_all[role, :, n * 512:(n + 1) * 512]).astype(BF16)
-                    for e4 in range(4):
-                        xy[pl.ds(pl.multiple_of(e4 * rows + role * cap, 16), cap), n * 512:(n + 1) * 512] = (
-                            xg[e4 * cap:(e4 + 1) * cap, :])
-                return 0
-
-            lax.fori_loop(0, 4, gather, 0)
-
-            def pair(pp, _):
-                e0 = g * 4 + pp * 2
-                for s in range(2):
-                    e = e0 + s
-                    xr = pl.ds(pl.multiple_of((pp * 2 + s) * rows, 16), rows)
-                    hr = pl.ds(pl.multiple_of(e * rows, 16), rows)
-                    gate_part(e)
-                    a_expert(e, 2 * s).wait()
-                    a_expert(e, 2 * s + 1).wait()
-                    swiglu(xy, xr, 2 * s, he, hr)
-
-                    @pl.when(e0 + 2 < el)
-                    def _():
-                        a_expert(e + 2, 2 * s).start()
-                        a_expert(e + 2, 2 * s + 1).start()
-
-                    @pl.when(e0 + 2 >= el)
-                    def _():
-                        a_shared(2 * s).start()
-                        a_shared(2 * s + 1).start()
-                return 0
-
-            lax.fori_loop(0, 2, pair, 0)
-            return 0
-
-        lax.fori_loop(0, el // 4, group, 0)
+        for role in range(4):
+            gather(0, 0, role)
+
+        def pair(p, _):
+            for s in range(2):
+                e = p * 2 + s
+                a_expert(e, 2 * s).wait()
+                a_expert(e, 2 * s + 1).wait()
+                gate_part(e)
+                swiglu(xy, slice(s * rows, (s + 1) * rows), 2 * s,
+                       he, pl.ds(pl.multiple_of(e * rows, 16), rows),
+                       [lambda role=role: gather(e + 1, 1 - s, role) for role in range(4)])
+
+                @pl.when(e + 2 < el)
+                def _():
+                    a_expert(e + 2, 2 * s).start()
+                    a_expert(e + 2, 2 * s + 1).start()
+            return 0
+
+        lax.fori_loop(0, el // 2, pair, 0)
 
         def c_diag(c):
-            return rcopy(sdiag.at[lax.rem(c, 2)], rdiag.at[c], cs_diag.at[c], cr_diag.at[c], sib)
+            return rcopy(sdiag.at[lax.rem(c, 2)], rdiag.at[lax.rem(c, ND)], cs_diag.at[c], cr_diag.at[c], sib)
 
         def c_sib(c):
             return rcopy(ssib.at[lax.rem(c, 2)], rsib.at[lax.rem(c, 2)], cs_sib.at[c], cr_sib.at[c], sib)
 
         def c_cross(c):
-            return rcopy(rdiag.at[c], rcross.at[c], cs_cross.at[c], cr_cross.at[c], cross)
+            return rcopy(rdiag.at[lax.rem(c, ND)], rcross.at[c], cs_cross.at[c], cr_cross.at[c], cross)
 
         def partial(role):
             yc = xy[:, role * CC:(role + 1) * CC]
-            return (_dot(comb[role, :, 0:rl], yc) + _dot(comb[role, :, rl:2 * rl], yc)
-                    + _dot(comb[role, :, 2 * rl:3 * rl], yc))
+            return _dot(comb[role], jnp.concatenate([yc, yc, yc], axis=0))
+
+        def add_sib(c):
+            c_sib(c).wait_recv()
+            macc[c] = macc[c] + rsib[lax.rem(c, 2)]
 
         def chunk(c, _):
-            def four(q, _):
-                i = c * (el // EB) + q
-                sl = lax.rem(i, NB)
-                b_ue2(i).wait()
-                for s in range(EB):
-                    e = q * EB + s
-                    y = _dot(he[pl.ds(pl.multiple_of(e * rows, 16), rows), :], ring_b[sl, s]).astype(BF16)
-                    for role in range(4):
-                        xy[pl.ds(pl.multiple_of(e * cap, 16), cap), role * CC:(role + 1) * CC] = (
-                            y[role * cap:(role + 1) * cap, :])
-
-                @pl.when(i + NB < nue2)
-                def _():
-                    b_ue2(i + NB).start()
-
-                @pl.when(i + NB >= nue2)
-                def _():
-                    for cp in b_ws2(i + NB):
-                        cp.start()
-                return 0
-
-            lax.fori_loop(0, el // EB, four, 0)
+            @pl.when(c >= 1)
+            def _():
+                add_sib(c - 1)
 
             @pl.when(c >= 2)
             def _():
                 c_diag(c - 2).wait_send()
                 c_sib(c - 2).wait_send()
 
+            @pl.when(c >= ND - 1)
+            def _():
+                c_cross(c - (ND - 1)).wait_send()
+
+            @pl.when((c >= 1) & (c <= 2 * nf))
+            def _():
+                for k in range(2 * nf):
+                    @pl.when(c == k + 1)
+                    def _():
+                        a_shared(k).start()
+
+            for blk in range(2):
+                slots = range(blk * (NB // 2), (blk + 1) * (NB // 2))
+                for sl in slots:
+                    b_ue2(c * NB + sl, sl).wait()
+                for sl in slots:
+                    for s in range(EB):
+                        e = sl * EB + s
+                        y = _dot(he[e * rows:(e + 1) * rows, :], ring_b[sl, s]).astype(BF16)
+                        for role in range(4):
+                            xy[e * cap:(e + 1) * cap, role * CC:(role + 1) * CC] = y[role * cap:(role + 1) * cap, :]
+
+                @pl.when(c + 1 < nch)
+                def _():
+                    for sl in slots:
+                        b_ue2((c + 1) * NB + sl, sl).start()
+
+                @pl.when(c + 1 == nch)
+                def _():
+                    for sl in slots:
+                        for cp in b_ws2(nue2 + sl, sl):
+                            cp.start()
+
             sdiag[lax.rem(c, 2)] = partial(DIAG)
+            ssib[lax.rem(c, 2)] = partial(SIB)
             c_diag(c).start()
-            ssib[lax.rem(c, 2)] = partial(SIB)
             c_sib(c).start()
+            pc = partial(CROSS)
             macc[c] = partial(OWN)
-            pc = partial(CROSS)
             c_diag(c).wait_recv()
-            rdiag[c] = rdiag[c] + pc
+            rdiag[lax.rem(c, ND)] = rdiag[lax.rem(c, ND)] + pc
             c_cross(c).start()
-            c_sib(c).wait_recv()
-            macc[c] = macc[c] + rsib[lax.rem(c, 2)]
             return 0
 
         lax.fori_loop(0, nch, chunk, 0)
+        add_sib(nch - 1)
 
         for half in range(nf):
             a_shared(2 * half).wait()
             a_shared(2 * half + 1).wait()
             swiglu(x1v, slice(0, t), 2 * half, he, slice(half * t, (half + 1) * t))
 
+        for k in range(nws2):
+            for cp in b_ws2(nue2 + k, k):
+                cp.wait()
+
         def shared_out(k, _):
-            i = k + nue2
-            for cp in b_ws2(i):
-                cp.wait()
             for u in range(cpt):
                 f = macc[k * cpt + u]
                 for half in range(nf):
-                    f = f + _dot(he[half * t:(half + 1) * t, :], ring_b[lax.rem(i, NB), u * nf + half])
+                    f = f + _dot(he[half * t:(half + 1) * t, :], ring_b[k, u * nf + half])
                 macc[k * cpt + u] = f
-
-            @pl.when(k + NB < nws2)
-            def _():
-                for cp in b_ws2(i + NB):
-                    cp.start()
             return 0
 
         lax.fori_loop(0, nws2, shared_out, 0)
@@ -394,7 +395,8 @@
             if c >= nch - 2:
                 c_diag(c).wait_send()
                 c_sib(c).wait_send()
-            c_cross(c).wait_send()
+            if c >= nch - (ND - 1):
+                c_cross(c).wait_send()
             pltpu.make_async_copy(x1v.at[:, pl.ds(c * CC, CC)], out_hbm.at[:, pl.ds(c * CC, CC)],
                                   sem_out.at[c]).wait()
 
@@ -418,11 +420,10 @@
             vm((t, d), BF16),
             vm((t, d), BF16),
             vm((4, 16, t), F32),
-            vm((4, t, 128), F32),
             vm((nch, t, CC), F32),
             vm((2, t, CC), F32),
             vm((nch, t, CC), F32),
-            vm((nch, t, CC), F32),
+            vm((ND, t, CC), F32),
             vm((2, t, CC), F32),
             vm((2, t, CC), F32),
             dma((NA,)), dma((NB, EB)), dma, dma((nch,)),

time: 159 us -> 147 us (0.925)
  Pallas kernels: 156 us -> 145 us
    pallas_call x1, Pallas kernels: 156 us -> 145 us  [local(): call(h0.reshape(t, d), *ids, *gains, cos, sin, wr.T, wq, wk, wv, wo, ws1,...]
where the time goes in v3:
time: 147 us
  Pallas kernels  145 us (99%)
  local copies, waits for them, and re-layouts  2.3 us (2%)
    pallas_call x1, Pallas kernels, local(): call(h0.reshape(t, d), *ids, *gains, cos, sin, wr.T, wq, wk, wv, wo, ws1,...  145 us

profile of v3, /device:TPU:0, one launch (start us, length us, event | category | flops | bytes accessed | tf_op | source)
XLA Modules:
  0.0 147.3 jit_solution(12435480240557763542)
XLA Ops:
  0.0 145.0 %moe_layer.1 = bf16[256,2048]{1,0:T(8,128)(2,1)} custom-call(bf16[256,2048]{1,0:T(8,128)(2,1)} %bitcast.9, s32[6,1,256]{2,1,0:T(1,128)} %bitcast.11, s32[6,1,256]{2,1,0:T(1,128)} %bitcast.12, bf16[16,128]{1,0:T(8,128)(2,1)} %bitcast.13, bf16[16,128]{1,0:T(8,128)(2,1)} %bitcast.14, bf16[16,128]{1,0:T(8,128)(2,1)} %bitcast.15, ...), custom_call_target="tpu_custom_call" | custom-call | tf_op jit(solution)/shard_map/moe_layer/pallas_call | solution.py:455
  145.0 2.3 %copy.21 = bf16[1,256,2048]{2,1,0:T(8,128)(2,1)} copy(bf16[1,256,2048]{2,1,0:T(8,128)(2,1)} %bitcast.8) | data formatting | bytes 2097152

commit v4 on v3

v4 whole, which is shorter than its diff:
```python
import jax
import jax.numpy as jnp
import numpy as np
from jax import lax
from jax.experimental import pallas as pl
from jax.experimental.pallas import tpu as pltpu
from jax.sharding import PartitionSpec as P

MESH = pl.DeviceIdType.MESH
F32 = jnp.float32
BF16 = jnp.bfloat16
EPS = 1e-6
HEAD = 128
CAP_FACTOR = 2

OWN, SIB, CROSS, DIAG = range(4)
NA = 4
NB = 4
EB = 4
CC = 256
UC = 4


def _dot(a, b):
    return jnp.dot(a, b, preferred_element_type=F32)


def _rope_tables(s):
    half = HEAD // 2
    freq = np.float32(10000.0) ** (-np.arange(half, dtype=np.float32) / np.float32(half))
    ang = np.arange(s, dtype=np.float32)[:, None] * freq.astype(np.float32)[None, :]
    c, sn = np.cos(ang), np.sin(ang)
    return np.concatenate([c, c], 1).astype(np.float32), np.concatenate([-sn, sn], 1).astype(np.float32)


def _build(t, d, fe, fs, el, cap, top):
    nh = d // HEAD
    rows = 4 * cap
    rl = el * cap
    nch = d // CC
    uc = t // UC
    nta = 8 + 2 * el
    nue2 = nch * el // EB
    dh = d // 2
    fh = fe // 2 // 256 * 256 + 256
    nf = fs // fe
    cpt = EB // nf
    nws2 = nch // cpt
    assert el == NB * EB and nws2 == NB

    def kernel(h0_hbm, idx_hbm, slot_hbm, lna_hbm, lnf_hbm, lnm_hbm, cos_hbm, sin_hbm, wr_hbm, wq, wk, wv, wo, ws1, ws3, ws2,
               ue1, ue3, ue2, out_hbm,
               idx_ref, slot_ref, gain_ref,
               ring_a, ring_b, u_all, comb, xbuf, ybuf, he, ln_ref, h0v, mrow,
               macc, rsib, rcross, rdiag, sdiag, ssib, pcs,
               sem_a, sem_b, sem_in, sem_small, sem_out,
               ms, mr, us_sib, ur_sib, us_cross, ur_cross, us_fwd, ur_diag,
               cs_diag, cr_diag, cs_sib, cr_sib, cs_cross, cr_cross):
        me = lax.axis_index('ep')
        core = lax.rem(me, 2)
        sib = me + 1 - 2 * core
        cross = lax.rem(me + 2, 4)
        diag = lax.rem(sib + 2, 4)
        base = (me * rl).astype(F32)

        def rcopy(src, dst, ssem, rsem, dev):
            return pltpu.make_async_remote_copy(src_ref=src, dst_ref=dst, send_sem=ssem, recv_sem=rsem,
                                                device_id={'ep': dev}, device_id_type=MESH)

        def a_dense(k):
            w = (wq, wk, wv, wo)[k // 2]
            return pltpu.make_async_copy(w.at[:, pl.ds((k % 2) * (d // 2), d // 2)],
                                         ring_a.at[k % NA, :, pl.ds(0, d // 2)], sem_a.at[k % NA, 0])

        def a_expert(e, s, h):
            cols = pl.ds(h * fh, (fh, fe - fh)[h])
            return pltpu.make_async_copy((ue1, ue3)[s % 2].at[e, :, cols], ring_a.at[s, :, cols], sem_a.at[s, h])

        def a_shared(k):
            return pltpu.make_async_copy((ws1, ws3)[k % 2].at[:, pl.ds((k // 2) * fe, fe)],
                                         ring_a.at[k], sem_a.at[k, 0])

        def b_ue2(i, sl):
            e0 = lax.rem(i, el // EB) * EB
            col = pl.multiple_of(lax.div(i, el // EB) * CC, CC)
            return pltpu.make_async_copy(ue2.at[pl.ds(e0, EB), :, pl.ds(col, CC)], ring_b.at[sl], sem_b.at[sl, 0])

        def b_ws2(i, sl):
            k = i - nue2
            return [pltpu.make_async_copy(
                ws2.at[pl.ds(half * fe, fe), pl.ds(pl.multiple_of((k * cpt + u) * CC, CC), CC)],
                ring_b.at[sl, u * nf + half], sem_b.at[sl, u * nf + half])
                for u in range(cpt) for half in range(nf)]

        h0_in = [pltpu.make_async_copy(h0_hbm.at[pl.ds(i * uc, uc)], h0v.at[pl.ds(i * uc, uc)], sem_in.at[i])
                 for i in range(UC)]
        small = [pltpu.make_async_copy(a, b, sem_small.at[i]) for i, (a, b) in enumerate((
            (lna_hbm, gain_ref.at[0]), (lnf_hbm, gain_ref.at[1]), (lnm_hbm, gain_ref.at[2]), (idx_hbm, idx_ref),
            (slot_hbm, slot_ref), (wr_hbm, xbuf.at[pl.ds(0, el * 4)]), (cos_hbm, macc.at[4, :, pl.ds(0, HEAD)]),
            (sin_hbm, macc.at[5, :, pl.ds(0, HEAD)])))]
        for cp in small[:3] + h0_in + small[3:]:
            cp.start()
        bar = pltpu.get_barrier_semaphore()
        for dev in (sib, cross, diag):
            pl.semaphore_signal(bar, inc=1, device_id={'ep': dev}, device_id_type=MESH)
        for k in range(3):
            small[k].wait()
        for k in range(3):
            w = gain_ref[k].astype(F32)
            for i in range(d // 128):
                ln_ref[k:k + 1, i * 128:(i + 1) * 128] = w[i:i + 1, :]

        def u_sib(i):
            r = pl.ds(i * uc, uc)
            return rcopy(u_all.at[OWN, r], u_all.at[SIB, r], us_sib.at[i], ur_sib.at[i], sib)

        def u_cross(i):
            r = pl.ds(i * uc, uc)
            return rcopy(u_all.at[OWN, r], u_all.at[CROSS, r],
                         us_cross.at[i], ur_cross.at[i], cross)

        def u_fwd(i):
            r = pl.ds(i * uc, uc)
            return rcopy(u_all.at[CROSS, r], u_all.at[DIAG, r],
                         us_fwd.at[i], ur_diag.at[i], sib)

        def relay(i):
            u_cross(i).wait_recv()
            u_fwd(i).start()

        def norm_in(k, _):
            r = pl.ds(pl.multiple_of(k * 16, 16), 16)
            x = h0v[r, :].astype(F32)
            n = x * lax.rsqrt(jnp.mean(x * x, axis=-1, keepdims=True) + EPS)
            u_all[OWN, r, :] = (n * ln_ref[2:3, :]).astype(BF16)
            x1 = (n * ln_ref[0:1, :]).astype(BF16)
            for half in range(2):
                he[pl.ds(pl.multiple_of((6 + half) * t + k * 16, 16), 16), 0:dh] = x1[:, half * dh:(half + 1) * dh]
            return 0

        def halves(k):
            return jnp.concatenate([he[k * t:(k + 1) * t, 0:dh], he[(k + 1) * t:(k + 2) * t, 0:dh]], axis=1)

        for i in range(UC):
            h0_in[i].wait()
            if i == 1:
                for k in range(NA):
                    a_dense(k).start()
            lax.fori_loop(i * uc // 16, (i + 1) * uc // 16, norm_in, 0)
            if i == 0:
                pl.semaphore_wait(bar, 3)
            if i < UC // 2:
                u_cross(i).start()
                u_sib(i).start()
        for k in range(3, 8):
            small[k].wait()

        lg = lax.dot_general(xbuf[0:el * 4, :], u_all[OWN], (((1,), (1,)), ((), ())), preferred_element_type=F32)
        ex = lax.broadcasted_iota(jnp.int32, lg.shape, 0)
        lj = [jnp.sum(jnp.where(ex == idx_ref[j], lg, 0.0), axis=0, keepdims=True) for j in range(top)]
        mx = lj[0]
        for j in range(1, top):
            mx = jnp.maximum(mx, lj[j])
        ej = [jnp.exp(v - mx) for v in lj]
        tot = ej[0]
        for j in range(1, top):
            tot = tot + ej[j]
        mrow[OWN] = jnp.zeros((16, t), F32)
        for j in range(top):
            mrow[OWN, j:j + 1, :] = (idx_ref[j] * cap + slot_ref[j]).astype(F32)
            mrow[OWN, 8 + j:9 + j, :] = ej[j] / tot
        m_copies = [rcopy(mrow.at[OWN], mrow.at[role], ms.at[role - 1], mr.at[role - 1], dev)
                    for role, dev in ((SIB, sib), (CROSS, cross), (DIAG, diag))]
        for c in m_copies:
            c.start()
        for i in range(UC // 2, UC):
            u_cross(i).start()
            u_sib(i).start()

        def qkv(k, rope):
            a_dense(k).wait()

            for n in range(2):
                y = _dot(halves(6), ring_a[k % NA, :, n * 512:(n + 1) * 512])
                for h in range(4):
                    yh = y[:, h * HEAD:(h + 1) * HEAD]
                    if rope:
                        yh = yh * macc[4, :, 0:HEAD] + pltpu.roll(yh, HEAD // 2, 1) * macc[5, :, 0:HEAD]
                    col = n * 512 + h * HEAD
                    he[k * t:(k + 1) * t, col:col + HEAD] = yh.astype(BF16)

        for k in range(6):
            qkv(k, k < 4)
            if k < 4:
                a_dense(k + NA).start()
            else:
                a_expert(0, k % NA, 0).start()
                a_expert(0, k % NA, 1).start()
        relay(0)
        for i in range(NB):
            b_ue2(i, i).start()

        ri = lax.broadcasted_iota(jnp.int32, (t, t), 0)
        ci = lax.broadcasted_iota(jnp.int32, (t, t), 1)

        def head_pair(hp, _):
            for s in range(2):
                half = lax.div(hp, nh // 4)
                col = pl.ds(pl.multiple_of((lax.rem(hp, nh // 4) * 2 + s) * HEAD, HEAD), HEAD)
                rq, rk, rv = (pl.ds(pl.multiple_of((2 * kind + half) * t, t), t) for kind in range(3))
                q = he[rq, col]
                kk = he[rk, col]
                vv = he[rv, col]
                sc = lax.dot_general(q, kk, (((1,), (1,)), ((), ())), preferred_element_type=F32) * HEAD ** -0.5
                sc = jnp.where(ri >= ci, sc, -1e30)
                p = jnp.exp(sc - jnp.max(sc, axis=-1, keepdims=True))
                p = (p / jnp.sum(p, axis=-1, keepdims=True)).astype(BF16)
                he[rq, col] = _dot(p, vv).astype(BF16)
            return 0

        lax.fori_loop(0, nh // 2, head_pair, 0)
        relay(1)

        for k in (6, 7):
            a_dense(k).wait()

            for n in range(2):
                col = slice((k % 2) * (d // 2) + n * 512, (k % 2) * (d // 2) + (n + 1) * 512)
                y = _dot(halves(0), ring_a[k % NA, :, n * 512:(n + 1) * 512])
                h0v[:, col] = (h0v[:, col].astype(F32) + y).astype(BF16)
            a_expert(1, k % NA, 0).start()
            a_expert(1, k % NA, 1).start()

        for c in m_copies:
            c.wait()
        for role in range(4):
            macc[role, :, 0:128] = jnp.transpose(jnp.concatenate([mrow[role], jnp.zeros((112, t), F32)], axis=0))
        for i in range(2, UC):
            relay(i)
        for i in range(UC):
            u_sib(i).wait()
        for sl in range(NB):
            b_ue2(sl, sl).wait()

        def swiglu(lhs, sl, dr, between=()):
            between = list(between)
            for n0 in range(0, fe - fe % 256, 256):
                cols = slice(n0, n0 + 256)
                y1 = _dot(lhs(), ring_a[sl, :, cols])
                y3 = _dot(lhs(), ring_a[sl + 1, :, cols])
                he[dr, cols] = (y1 * jax.nn.sigmoid(y1) * y3).astype(BF16)
                if between:
                    between.pop(0)()
            if fe % 256:
                cols = slice(fe - fe % 256, fe)
                y = _dot(lhs(), jnp.concatenate([ring_a[sl, :, cols], ring_a[sl + 1, :, cols]], axis=1))
                y1, y3 = y[:, :fe % 256], y[:, fe % 256:]
                he[dr, cols] = (y1 * jax.nn.sigmoid(y1) * y3).astype(BF16)

        def gather(e, buf, role):
            rr = (lax.broadcasted_iota(jnp.int32, (cap, t), 0) + e * cap).astype(F32) + base
            hit = rr == mrow[role, 0:1, :]
            for j in range(1, top):
                hit = hit | (rr == mrow[role, j:j + 1, :])
            oh = jnp.where(hit, 1.0, 0.0).astype(BF16)
            r0 = buf * rows + role * cap
            for n in range(d // 512):
                xbuf[r0:r0 + cap, n * 512:(n + 1) * 512] = _dot(oh, u_all[role, :, n * 512:(n + 1) * 512]).astype(BF16)

        npart = 4 * t // el
        def gate_part(i):
            role = lax.div(i, el // 4)
            r = pl.ds(pl.multiple_of(lax.rem(i, el // 4) * npart, npart), npart)
            for b in range(rl // 256):
                rr = (lax.broadcasted_iota(jnp.int32, (npart, 256), 1) + b * 256).astype(F32) + base
                w = jnp.zeros((npart, 256), F32)
                for j in range(top):
                    w = jnp.where(rr == macc[role, r, j:j + 1], macc[role, r, 8 + j:9 + j], w)
                for part in range(3):
                    piece = w.astype(BF16)
                    comb[role, r, part * rl + b * 256:part * rl + (b + 1) * 256] = piece
                    w = w - piece.astype(F32)

        for role in (OWN, SIB, CROSS):
            gather(0, 0, role)
        for i in range(UC):
            u_cross(i).wait_send()
            u_fwd(i).wait()
        gather(0, 0, DIAG)

        def y_first(e):
            y = _dot(he[pl.ds(pl.multiple_of(e * rows, 16), rows), :], ring_b[lax.div(e, EB), lax.rem(e, EB)])
            y = y.astype(BF16)
            for role in range(4):
                ybuf[pl.ds(pl.multiple_of(e * cap, 16), cap), role * CC:(role + 1) * CC] = y[role * cap:(role + 1) * cap, :]

        def expert(e, s, last):
            sls = (2 * s, 2 * s + 1)
            for h in range(1 if last else 2):
                for sl in sls:
                    a_expert(e, sl, h).wait()
            y_first(e - 1 if isinstance(e, int) else jnp.maximum(e - 1, 0))
            gate_part(e)

            def refill(h):
                for sl in sls:
                    a_expert(e + 2, sl, h).start()

            def step(k):
                if not last or s == 0:
                    gather(e + 1, 1 - s, k)
                if (k + 1) * 256 == fh:
                    if last:
                        for sl in sls:
                            a_expert(e, sl, 1).wait()
                    else:
                        refill(0)

            swiglu(lambda: xbuf[s * rows:(s + 1) * rows, :], 2 * s, pl.ds(pl.multiple_of(e * rows, 16), rows),
                   [lambda k=k: step(k) for k in range(4)])
            if not last:
                refill(1)

        def pair(p, _):
            for s in range(2):
                expert(p * 2 + s, s, False)
            return 0

        lax.fori_loop(0, el // 2 - 1, pair, 0)
        for sl in range(NB - 1):
            b_ue2(NB + sl, sl).start()
        for s in range(2):
            expert(el - 2 + s, s, True)

        def norm_a(c):
            nr = t // nch
            r = pl.ds(pl.multiple_of(c * nr, nr), nr)
            x = h0v[r, :].astype(F32)
            n = x * lax.rsqrt(jnp.mean(x * x, axis=-1, keepdims=True) + EPS)
            u_all[0, r, :] = (n * ln_ref[1:2, :]).astype(BF16)

        def c_diag(c):
            return rcopy(sdiag, rdiag.at[c], cs_diag.at[c], cr_diag.at[c], sib)

        def c_sib(c):
            return rcopy(ssib, rsib.at[lax.rem(c, 2)], cs_sib.at[c], cr_sib.at[c], sib)

        def c_cross(c):
            return rcopy(rdiag.at[c], rcross.at[c], cs_cross.at[c], cr_cross.at[c], cross)

        def partial(role):
            yc = ybuf[:, role * CC:(role + 1) * CC]
            return _dot(comb[role], jnp.concatenate([yc, yc, yc], axis=0))

        def exchange(c):
            sdiag[...] = partial(DIAG)
            ssib[...] = partial(SIB)
            c_diag(c).start()
            c_sib(c).start()
            pcs[...] = partial(CROSS)
            macc[c] = partial(OWN)

        def finish(c):
            c_diag(c).wait_recv()
            rdiag[c] = rdiag[c] + pcs[...]
            c_cross(c).start()
            c_sib(c).wait_recv()
            macc[c] = macc[c] + rsib[lax.rem(c, 2)]

        def chunk(c, _):
            @pl.when(c <= 2 * nf)
            def _():
                for k in range(2 * nf):
                    @pl.when(c == k + 1)
                    def _():
                        a_shared(k).start()

            for blk in range(2):
                slots = range(blk * (NB // 2), (blk + 1) * (NB // 2))
                for sl in slots:
                    b_ue2(c * NB + sl, sl).wait()
                if blk == 1:
                    norm_a(c)
                for sl in slots:
                    for s in range(EB):
                        e = sl * EB + s
                        y = _dot(he[e * rows:(e + 1) * rows, :], ring_b[sl, s]).astype(BF16)
                        for role in range(4):
                            ybuf[e * cap:(e + 1) * cap, role * CC:(role + 1) * CC] = y[role * cap:(role + 1) * cap, :]

                @pl.when(c + 1 < nch)
                def _():
                    for sl in slots:
                        b_ue2((c + 1) * NB + sl, sl).start()

                @pl.when(c + 1 == nch)
                def _():
                    for sl in slots:
                        for cp in b_ws2(nue2 + sl, sl):
                            cp.start()

                if blk == 0:
                    @pl.when(c >= 2)
                    def _():
                        finish(c - 1)

            c_diag(c - 1).wait_send()
            c_sib(c - 1).wait_send()
            exchange(c)

            @pl.when(c == nch - 1)
            def _():
                finish(c)
            return 0

        y_first(el - 1)
        norm_a(0)
        b_ue2(2 * NB - 1, NB - 1).start()
        exchange(0)
        finish(0)
        lax.fori_loop(1, nch, chunk, 0)

        for half in range(nf):
            a_shared(2 * half).wait()
            a_shared(2 * half + 1).wait()
            swiglu(lambda: u_all[0], 2 * half, slice(half * t, (half + 1) * t))

        for k in range(nws2):
            for cp in b_ws2(nue2 + k, k):
                cp.wait()

        def shared_out(k, _):
            for u in range(cpt):
                f = macc[k * cpt + u]
                for half in range(nf):
                    f = f + _dot(he[half * t:(half + 1) * t, :], ring_b[k, u * nf + half])
                macc[k * cpt + u] = f
            return 0

        lax.fori_loop(0, nws2, shared_out, 0)
        for c in range(nch):
            cols = slice(c * CC, (c + 1) * CC)
            c_cross(c).wait_recv()

            def fin(k, _):
                r = pl.ds(pl.multiple_of(k * 32, 32), 32)
                u_all[1, r, cols] = (h0v[r, cols].astype(F32) + macc[c, r] + rcross[c, r]).astype(BF16)
                return 0

            lax.fori_loop(0, t // 32, fin, 0)
            pltpu.make_async_copy(u_all.at[1, :, pl.ds(c * CC, CC)], out_hbm.at[:, pl.ds(c * CC, CC)],
                                  sem_out.at[c]).start()
        for c in range(nch):
            if c == nch - 1:
                c_diag(c).wait_send()
                c_sib(c).wait_send()
            c_cross(c).wait_send()
            pltpu.make_async_copy(u_all.at[1, :, pl.ds(c * CC, CC)], out_hbm.at[:, pl.ds(c * CC, CC)],
                                  sem_out.at[c]).wait()

    dma = pltpu.SemaphoreType.DMA
    vm = pltpu.VMEM
    any_ = pl.BlockSpec(memory_space=pl.ANY)
    return pl.pallas_call(
        kernel,
        out_shape=jax.ShapeDtypeStruct((t, d), BF16),
        in_specs=[any_] * 19,
        out_specs=any_,
        scratch_shapes=[
            vm((top, 1, t), jnp.int32), vm((top, 1, t), jnp.int32),
            vm((3, d // 128, 128), BF16),
            vm((NA, d, fe), BF16),
            vm((NB, EB, fe, CC), BF16),
            vm((4, t, d), BF16),
            vm((4, t, 3 * rl), BF16),
            vm((2 * rows, d), BF16),
            vm((rl, 4 * CC), BF16),
            vm((el * rows, fe), BF16),
            vm((8, d), F32),
            vm((t, d), BF16),
            vm((4, 16, t), F32),
            vm((nch, t, CC), F32),
            vm((2, t, CC), F32),
            vm((nch, t, CC), F32),
            vm((nch, t, CC), F32),
            vm((t, CC), F32),
            vm((t, CC), F32),
            vm((t, CC), F32),
            dma((NA, 2)), dma((NB, EB)), dma((UC,)), dma((8,)), dma((nch,)),
            dma((3,)), dma((3,)),
            dma((UC,)), dma((UC,)), dma((UC,)), dma((UC,)), dma((UC,)), dma((UC,)),
            dma((nch,)), dma((nch,)), dma((nch,)), dma((nch,)), dma((nch,)), dma((nch,)),
        ],
        compiler_params=pltpu.CompilerParams(collective_id=0, has_side_effects=True,
                                             vmem_limit_bytes=67043328),
        name='moe_layer',
    )


def solution(mesh):
    g_ = mesh.shape['ep']
    rows = P(('dp', 'ep'))
    rep = P()

    def local(h0, idx, slot, ln_attn, wq, wk, wv, wo, ln_ffn, ws1, ws3, ws2, ln_moe, wr, ue1, ue3, ue2):
        b, s, d = h0.shape
        top = idx.shape[-1]
        el, _, fe = ue1.shape
        t = b * s
        cap = CAP_FACTOR * t * top // (el * g_)
        cos, sin = _rope_tables(s)
        gains = [w.reshape(d // 128, 128) for w in (ln_attn, ln_ffn, ln_moe)]
        ids = [jnp.transpose(a, (2, 0, 1)).reshape(top, 1, t) for a in (idx, slot)]
        call = _build(t, d, fe, ws1.shape[1], el, cap, top)
        out = call(h0.reshape(t, d), *ids, *gains, cos, sin, wr.T,
                   wq, wk, wv, wo, ws1, ws3, ws2, ue1, ue3, ue2)
        return out.reshape(b, s, d)

    specs = (rows, rows, rows) + (rep,) * 11 + (P('ep'), P('ep'), P('ep'))
    return jax.shard_map(local, mesh=mesh, in_specs=specs, out_specs=rows, check_vma=False)
```

time: 147 us -> 141 us (0.959)
  Pallas kernels: 145 us -> 139 us
    pallas_call x1, Pallas kernels: 145 us -> 139 us  [local(): call(h0.reshape(t, d), *ids, *gains, cos, sin, wr.T, wq, wk, wv, wo, ws1,...]
where the time goes in v4:
time: 141 us
  Pallas kernels  139 us (99%)
  local copies, waits for them, and re-layouts  2.3 us (2%)
    pallas_call x1, Pallas kernels, local(): call(h0.reshape(t, d), *ids, *gains, cos, sin, wr.T, wq, wk, wv, wo, ws1,...  139 us

profile of v4, /device:TPU:0, one launch (start us, length us, event | category | flops | bytes accessed | tf_op | source)
XLA Modules:
  0.0 141.0 jit_solution(6523257862304487212)
XLA Ops:
  0.0 138.7 %moe_layer.1 = bf16[256,2048]{1,0:T(8,128)(2,1)} custom-call(bf16[256,2048]{1,0:T(8,128)(2,1)} %bitcast.9, s32[6,1,256]{2,1,0:T(1,128)} %bitcast.11, s32[6,1,256]{2,1,0:T(1,128)} %bitcast.12, bf16[16,128]{1,0:T(8,128)(2,1)} %bitcast.13, bf16[16,128]{1,0:T(8,128)(2,1)} %bitcast.14, bf16[16,128]{1,0:T(8,128)(2,1)} %bitcast.15, ...), custom_call_target="tpu_custom_call" | custom-call | tf_op jit(solution)/shard_map/moe_layer/pallas_call | solution.py:515
  138.7 2.3 %copy.21 = bf16[1,256,2048]{2,1,0:T(8,128)(2,1)} copy(bf16[1,256,2048]{2,1,0:T(8,128)(2,1)} %bitcast.8) | data formatting | bytes 2097152

commit v5 on v4

--- a/solution.py
+++ b/solution.py
@@ -169,10 +169,10 @@
         for j in range(top):
             mrow[OWN, j:j + 1, :] = (idx_ref[j] * cap + slot_ref[j]).astype(F32)
             mrow[OWN, 8 + j:9 + j, :] = ej[j] / tot
-        m_copies = [rcopy(mrow.at[OWN], mrow.at[role], ms.at[role - 1], mr.at[role - 1], dev)
-                    for role, dev in ((SIB, sib), (CROSS, cross), (DIAG, diag))]
-        for c in m_copies:
-            c.start()
+        m_sib, m_cross, m_fwd = [rcopy(mrow.at[a], mrow.at[b], ms.at[b - 1], mr.at[b - 1], dev)
+                                 for a, b, dev in ((OWN, SIB, sib), (OWN, CROSS, cross), (CROSS, DIAG, sib))]
+        m_cross.start()
+        m_sib.start()
         for i in range(UC // 2, UC):
             u_cross(i).start()
             u_sib(i).start()
@@ -219,7 +219,32 @@
             return 0
 
         lax.fori_loop(0, nh // 2, head_pair, 0)
+        m_cross.wait_recv()
+        m_fwd.start()
         relay(1)
+
+        def onehot(e, role):
+            rr = (lax.broadcasted_iota(jnp.int32, (cap, t), 0) + e * cap).astype(F32) + base
+            hit = rr == mrow[role, 0:1, :]
+            for j in range(1, top):
+                hit = hit | (rr == mrow[role, j:j + 1, :])
+            return jnp.where(hit, 1.0, 0.0).astype(BF16)
+
+        def gather(e, buf, role):
+            oh = onehot(e, role)
+            r0 = buf * rows + role * cap
+            for n in range(d // 512):
+                xbuf[r0:r0 + cap, n * 512:(n + 1) * 512] = _dot(oh, u_all[role, :, n * 512:(n + 1) * 512]).astype(BF16)
+
+        def gather_first(role):
+            oh = jnp.concatenate([onehot(0, role)] + [onehot(2 * p + 1, role) for p in range(el // 2)], axis=0)
+            for n in range(d // 512):
+                x = _dot(oh, u_all[role, :, n * 512:(n + 1) * 512]).astype(BF16)
+                xbuf[role * cap:(role + 1) * cap, n * 512:(n + 1) * 512] = x[0:cap, :]
+                half, col = divmod(n * 512, dh)
+                for p in range(el // 2):
+                    r0 = (2 * p + half) * rows + role * cap
+                    he[r0:r0 + cap, col:col + 512] = x[(p + 1) * cap:(p + 2) * cap, :]
 
         for k in (6, 7):
             a_dense(k).wait()
@@ -231,14 +256,18 @@
             a_expert(1, k % NA, 0).start()
             a_expert(1, k % NA, 1).start()
 
-        for c in m_copies:
-            c.wait()
+        m_sib.wait()
+        m_cross.wait_send()
+        m_fwd.wait()
         for role in range(4):
             macc[role, :, 0:128] = jnp.transpose(jnp.concatenate([mrow[role], jnp.zeros((112, t), F32)], axis=0))
-        for i in range(2, UC):
+        for i in range(2, UC - 1):
             relay(i)
         for i in range(UC):
             u_sib(i).wait()
+        gather_first(OWN)
+        gather_first(SIB)
+        relay(UC - 1)
         for sl in range(NB):
             b_ue2(sl, sl).wait()
 
@@ -253,19 +282,10 @@
                     between.pop(0)()
             if fe % 256:
                 cols = slice(fe - fe % 256, fe)
-                y = _dot(lhs(), jnp.concatenate([ring_a[sl, :, cols], ring_a[sl + 1, :, cols]], axis=1))
+                y = sum(_dot(lhs()[:, k:k + dh], jnp.concatenate(
+                    [ring_a[sl, k:k + dh, cols], ring_a[sl + 1, k:k + dh, cols]], axis=1)) for k in (0, dh))
                 y1, y3 = y[:, :fe % 256], y[:, fe % 256:]
                 he[dr, cols] = (y1 * jax.nn.sigmoid(y1) * y3).astype(BF16)
-
-        def gather(e, buf, role):
-            rr = (lax.broadcasted_iota(jnp.int32, (cap, t), 0) + e * cap).astype(F32) + base
-            hit = rr == mrow[role, 0:1, :]
-            for j in range(1, top):
-                hit = hit | (rr == mrow[role, j:j + 1, :])
-            oh = jnp.where(hit, 1.0, 0.0).astype(BF16)
-            r0 = buf * rows + role * cap
-            for n in range(d // 512):
-                xbuf[r0:r0 + cap, n * 512:(n + 1) * 512] = _dot(oh, u_all[role, :, n * 512:(n + 1) * 512]).astype(BF16)
 
         npart = 4 * t // el
         def gate_part(i):
@@ -281,16 +301,16 @@
                     comb[role, r, part * rl + b * 256:part * rl + (b + 1) * 256] = piece
                     w = w - piece.astype(F32)
 
-        for role in (OWN, SIB, CROSS):
-            gather(0, 0, role)
+        gather_first(CROSS)
         for i in range(UC):
             u_cross(i).wait_send()
             u_fwd(i).wait()
-        gather(0, 0, DIAG)
+        gather_first(DIAG)
 
         def y_first(e):
-            y = _dot(he[pl.ds(pl.multiple_of(e * rows, 16), rows), :], ring_b[lax.div(e, EB), lax.rem(e, EB)])
-            y = y.astype(BF16)
+            er = pl.ds(pl.multiple_of(e * rows, 16), rows)
+            y = sum(_dot(he[er, a:b], ring_b[lax.div(e, EB), lax.rem(e, EB), a:b, :])
+                    for a, b in ((0, fh), (fh, fe))).astype(BF16)
             for role in range(4):
                 ybuf[pl.ds(pl.multiple_of(e * cap, 16), cap), role * CC:(role + 1) * CC] = y[role * cap:(role + 1) * cap, :]
 
@@ -299,6 +319,10 @@
             for h in range(1 if last else 2):
                 for sl in sls:
                     a_expert(e, sl, h).wait()
+            if s == 0:
+                for half in range(2):
+                    xbuf[rows:2 * rows, half * dh:(half + 1) * dh] = (
+                        he[pl.ds(pl.multiple_of((e + half) * rows, 16), rows), 0:dh])
             y_first(e - 1 if isinstance(e, int) else jnp.maximum(e - 1, 0))
             gate_part(e)
 
@@ -307,8 +331,8 @@
                     a_expert(e + 2, sl, h).start()
 
             def step(k):
-                if not last or s == 0:
-                    gather(e + 1, 1 - s, k)
+                if s == 1 and not last:
+                    gather(e + 1, 0, k)
                 if (k + 1) * 256 == fh:
                     if last:
                         for sl in sls:
@@ -400,7 +424,7 @@
                             cp.start()
 
                 if blk == 0:
-                    @pl.when(c >= 2)
+                    @pl.when(c >= 3)
                     def _():
                         finish(c - 1)
 
@@ -408,16 +432,16 @@
             c_sib(c - 1).wait_send()
             exchange(c)
 
-            @pl.when(c == nch - 1)
+            @pl.when((c == 1) | (c == nch - 1))
             def _():
                 finish(c)
             return 0
 
         y_first(el - 1)
-        norm_a(0)
         b_ue2(2 * NB - 1, NB - 1).start()
         exchange(0)
         finish(0)
+        norm_a(0)
         lax.fori_loop(1, nch, chunk, 0)
 
         for half in range(nf):

time: 141 us -> 138 us (0.979)
  Pallas kernels: 139 us -> 135 us
    pallas_call x1, Pallas kernels: 139 us -> 135 us  [local(): call(h0.reshape(t, d), *ids, *gains, cos, sin, wr.T, wq, wk, wv, wo, ws1,...]
where the time goes in v5:
time: 138 us; the launch traced here: 137 us
  Pallas kernels  135 us (98%)
  local copies, waits for them, and re-layouts  2.3 us (2%)
    pallas_call x1, Pallas kernels, local(): call(h0.reshape(t, d), *ids, *gains, cos, sin, wr.T, wq, wk, wv, wo, ws1,...  135 us

profile of v5, /device:TPU:0, one launch (start us, length us, event | category | flops | bytes accessed | tf_op | source)
XLA Modules:
  0.0 137.4 jit_solution(16712214803236906611)
XLA Ops:
  0.0 135.1 %moe_layer.1 = bf16[256,2048]{1,0:T(8,128)(2,1)} custom-call(bf16[256,2048]{1,0:T(8,128)(2,1)} %bitcast.9, s32[6,1,256]{2,1,0:T(1,128)} %bitcast.11, s32[6,1,256]{2,1,0:T(1,128)} %bitcast.12, bf16[16,128]{1,0:T(8,128)(2,1)} %bitcast.13, bf16[16,128]{1,0:T(8,128)(2,1)} %bitcast.14, bf16[16,128]{1,0:T(8,128)(2,1)} %bitcast.15, ...), custom_call_target="tpu_custom_call" | custom-call | tf_op jit(solution)/shard_map/moe_layer/pallas_call | solution.py:539
  135.1 2.3 %copy.21 = bf16[1,256,2048]{2,1,0:T(8,128)(2,1)} copy(bf16[1,256,2048]{2,1,0:T(8,128)(2,1)} %bitcast.8) | data formatting | bytes 2097152

commit v6 on v5

--- a/solution.py
+++ b/solution.py
@@ -316,7 +316,7 @@
 
         def expert(e, s, last):
             sls = (2 * s, 2 * s + 1)
-            for h in range(1 if last else 2):
+            for h in range(2):
                 for sl in sls:
                     a_expert(e, sl, h).wait()
             if s == 0:
@@ -333,12 +333,8 @@
             def step(k):
                 if s == 1 and not last:
                     gather(e + 1, 0, k)
-                if (k + 1) * 256 == fh:
-                    if last:
-                        for sl in sls:
-                            a_expert(e, sl, 1).wait()
-                    else:
-                        refill(0)
+                if (k + 1) * 256 == fh and not last:
+                    refill(0)
 
             swiglu(lambda: xbuf[s * rows:(s + 1) * rows, :], 2 * s, pl.ds(pl.multiple_of(e * rows, 16), rows),
                    [lambda k=k: step(k) for k in range(4)])
@@ -384,10 +380,12 @@
             pcs[...] = partial(CROSS)
             macc[c] = partial(OWN)
 
-        def finish(c):
+        def send_cross(c):
             c_diag(c).wait_recv()
             rdiag[c] = rdiag[c] + pcs[...]
             c_cross(c).start()
+
+        def add_sib(c):
             c_sib(c).wait_recv()
             macc[c] = macc[c] + rsib[lax.rem(c, 2)]
 
@@ -424,25 +422,28 @@
                             cp.start()
 
                 if blk == 0:
-                    @pl.when(c >= 3)
+                    @pl.when(c >= 4)
                     def _():
-                        finish(c - 1)
+                        send_cross(c - 1)
+
+                    add_sib(c - 1)
 
             c_diag(c - 1).wait_send()
             c_sib(c - 1).wait_send()
             exchange(c)
 
-            @pl.when((c == 1) | (c == nch - 1))
+            @pl.when((c <= 2) | (c == nch - 1))
             def _():
-                finish(c)
+                send_cross(c)
             return 0
 
         y_first(el - 1)
         b_ue2(2 * NB - 1, NB - 1).start()
         exchange(0)
-        finish(0)
+        send_cross(0)
         norm_a(0)
         lax.fori_loop(1, nch, chunk, 0)
+        add_sib(nch - 1)
 
         for half in range(nf):
             a_shared(2 * half).wait()

time: 138 us -> 137 us (level)
  no operation moved by 1% of the time
where the time goes in v6:
time: 137 us
  Pallas kernels  135 us (99%)
  local copies, waits for them, and re-layouts  2.3 us (2%)
    pallas_call x1, Pallas kernels, local(): call(h0.reshape(t, d), *ids, *gains, cos, sin, wr.T, wq, wk, wv, wo, ws1,...  135 us

profile of v6, /device:TPU:0, one launch (start us, length us, event | category | flops | bytes accessed | tf_op | source)
XLA Modules:
  0.0 137.0 jit_solution(11403504179437377370)
XLA Ops:
  0.0 134.7 %moe_layer.1 = bf16[256,2048]{1,0:T(8,128)(2,1)} custom-call(bf16[256,2048]{1,0:T(8,128)(2,1)} %bitcast.9, s32[6,1,256]{2,1,0:T(1,128)} %bitcast.11, s32[6,1,256]{2,1,0:T(1,128)} %bitcast.12, bf16[16,128]{1,0:T(8,128)(2,1)} %bitcast.13, bf16[16,128]{1,0:T(8,128)(2,1)} %bitcast.14, bf16[16,128]{1,0:T(8,128)(2,1)} %bitcast.15, ...), custom_call_target="tpu_custom_call" | custom-call | tf_op jit(solution)/shard_map/moe_layer/pallas_call | solution.py:540
  134.7 2.3 %copy.21 = bf16[1,256,2048]{2,1,0:T(8,128)(2,1)} copy(bf16[1,256,2048]{2,1,0:T(8,128)(2,1)} %bitcast.8) | data formatting | bytes 2097152

commit v7 on v6

--- a/solution.py
+++ b/solution.py
@@ -422,7 +422,7 @@
                             cp.start()
 
                 if blk == 0:
-                    @pl.when(c >= 4)
+                    @pl.when(c >= 5)
                     def _():
                         send_cross(c - 1)
 
@@ -432,7 +432,7 @@
             c_sib(c - 1).wait_send()
             exchange(c)
 
-            @pl.when((c <= 2) | (c == nch - 1))
+            @pl.when((c <= 3) | (c == nch - 1))
             def _():
                 send_cross(c)
             return 0

time: 137 us -> 137 us (level)
  no operation moved by 1% of the time
where the time goes in v7:
time: 137 us
  Pallas kernels  135 us (99%)
  local copies, waits for them, and re-layouts  2.3 us (2%)
    pallas_call x1, Pallas kernels, local(): call(h0.reshape(t, d), *ids, *gains, cos, sin, wr.T, wq, wk, wv, wo, ws1,...  135 us

profile of v7, /device:TPU:0, one launch (start us, length us, event | category | flops | bytes accessed | tf_op | source)
XLA Modules:
  0.0 137.0 jit_solution(12550480640202674674)
XLA Ops:
  0.0 134.7 %moe_layer.1 = bf16[256,2048]{1,0:T(8,128)(2,1)} custom-call(bf16[256,2048]{1,0:T(8,128)(2,1)} %bitcast.9, s32[6,1,256]{2,1,0:T(1,128)} %bitcast.11, s32[6,1,256]{2,1,0:T(1,128)} %bitcast.12, bf16[16,128]{1,0:T(8,128)(2,1)} %bitcast.13, bf16[16,128]{1,0:T(8,128)(2,1)} %bitcast.14, bf16[16,128]{1,0:T(8,128)(2,1)} %bitcast.15, ...), custom_call_target="tpu_custom_call" | custom-call | tf_op jit(solution)/shard_map/moe_layer/pallas_call | solution.py:540
  134.7 2.3 %copy.21 = bf16[1,256,2048]{2,1,0:T(8,128)(2,1)} copy(bf16[1,256,2048]{2,1,0:T(8,128)(2,1)} %bitcast.8) | data formatting | bytes 2097152
